TPU v7x, 32 devices: a whole 2x2x4 slice. The times are simulated.
32 devices in a mesh: model: 4 (over z), data: 8 (over y, x, core).
Axes of the slice: x: 2, y: 2, z: 4, core: 2. Of those that a mesh axis runs over, the one named last changes fastest.
Arguments:
- grad_qkv: float32 [8, 2, 1024, 3072], P('data', None, None, 'model')
- weight_qkv: float32 [2, 1024, 3072], P(None, 'data', 'model')
- moment1_qkv: float32 [2, 1024, 3072], P(None, 'data', 'model')
- moment2_qkv: float32 [2, 1024, 3072], P(None, 'data', 'model')
- grad_proj: float32 [8, 2, 1024, 1024], P('data', None, 'model')
- weight_proj: float32 [2, 1024, 1024], P(None, ('model', 'data'))
- moment1_proj: float32 [2, 1024, 1024], P(None, ('model', 'data'))
- moment2_proj: float32 [2, 1024, 1024], P(None, ('model', 'data'))
- grad_fcin: float32 [8, 2, 1024, 4096], P('data', None, None, 'model')
- weight_fcin: float32 [2, 1024, 4096], P(None, 'data', 'model')
- moment1_fcin: float32 [2, 1024, 4096], P(None, 'data', 'model')
- moment2_fcin: float32 [2, 1024, 4096], P(None, 'data', 'model')
- grad_fcout: float32 [8, 2, 4096, 1024], P('data', None, 'model')
- weight_fcout: float32 [2, 4096, 1024], P(None, ('model', 'data'))
- moment1_fcout: float32 [2, 4096, 1024], P(None, ('model', 'data'))
- moment2_fcout: float32 [2, 4096, 1024], P(None, ('model', 'data'))
Outputs:
- output 1: bfloat16 [2, 1024, 3072], P(None, None, 'model')
- output 2: bfloat16 [2, 1024, 1024], P(None, 'model')
- output 3: bfloat16 [2, 1024, 4096], P(None, None, 'model')
- output 4: bfloat16 [2, 4096, 1024], P(None, 'model')
- output 5: float32 [2, 1024, 3072], P(None, 'data', 'model')
- output 6: float32 [2, 1024, 1024], P(None, ('model', 'data'))
- output 7: float32 [2, 1024, 4096], P(None, 'data', 'model')
- output 8: float32 [2, 4096, 1024], P(None, ('model', 'data'))
- output 9: float32 [2, 1024, 3072], P(None, 'data', 'model')
- output 10: float32 [2, 1024, 1024], P(None, ('model', 'data'))
- output 11: float32 [2, 1024, 4096], P(None, 'data', 'model')
- output 12: float32 [2, 4096, 1024], P(None, ('model', 'data'))
- output 13: float32 [2, 1024, 3072], P(None, 'data', 'model')
- output 14: float32 [2, 1024, 1024], P(None, ('model', 'data'))
- output 15: float32 [2, 1024, 4096], P(None, 'data', 'model')
- output 16: float32 [2, 4096, 1024], P(None, ('model', 'data'))
All inputs are finite; a program needn't handle non-finite values.
Results may differ from a plain program's by a relative error of at most 0.001.
Values are sent between devices in bfloat16 or wider.
A program may use at most 1 GiB of HBM per device.

v0:
```python
import jax
import jax.numpy as jnp
from jax import lax
from jax.sharding import PartitionSpec as P

LEARN_RATE = 0.08
BETA_ONE = 0.9
BETA_TWO = 0.999
ADAM_EPS = 1e-6
DECAY_RATE = 0.01
MAX_NORM = 1.0
STEP_COUNT = 100
COLUMN_SPLIT = (True, False, True, False)


def grad_spec(col_split):
    return P("data", None, None, "model") if col_split else P("data", None, "model", None)


def state_spec(col_split):
    return P(None, "data", "model") if col_split else P(None, ("model", "data"), None)


def replica_spec(col_split):
    return P(None, None, "model") if col_split else P(None, "model", None)


def adam_direction(grad_mean, weight, moment1, moment2, clip_coef):
    clipped = clip_coef * grad_mean
    new_first = BETA_ONE * moment1 + (1.0 - BETA_ONE) * clipped
    new_second = BETA_TWO * moment2 + (1.0 - BETA_TWO) * clipped * clipped
    first_hat = new_first / (1.0 - BETA_ONE ** STEP_COUNT)
    second_hat = new_second / (1.0 - BETA_TWO ** STEP_COUNT)
    update = first_hat / (jnp.sqrt(second_hat) + ADAM_EPS) + DECAY_RATE * weight
    return update, new_first, new_second


def solution(mesh):
    group_size = mesh.shape["data"]
    in_specs = []
    for col_split in COLUMN_SPLIT:
        in_specs.extend([grad_spec(col_split), state_spec(col_split), state_spec(col_split), state_spec(col_split)])
    out_specs = tuple([replica_spec(col_split) for col_split in COLUMN_SPLIT] + [state_spec(col_split) for col_split in COLUMN_SPLIT] * 3)

    def device_step(*arrays):
        kind_count = len(COLUMN_SPLIT)
        grad_means = []
        for kind_idx in range(kind_count):
            sent_grad = arrays[4 * kind_idx].astype(jnp.bfloat16)
            received = lax.all_to_all(sent_grad, "data", 2, 0, tiled=True)
            grad_means.append(jnp.sum(received, axis=0, dtype=jnp.float32) / group_size)
        local_sq = sum(jnp.sum(grad_mean * grad_mean) for grad_mean in grad_means)
        total_norm = jnp.sqrt(lax.psum(local_sq, ("model", "data")))
        clip_coef = jnp.minimum(1.0, MAX_NORM / total_norm)
        replicas, weights, firsts, seconds = [], [], [], []
        for kind_idx in range(kind_count):
            weight = arrays[4 * kind_idx + 1]
            update, new_first, new_second = adam_direction(grad_means[kind_idx], weight, arrays[4 * kind_idx + 2], arrays[4 * kind_idx + 3], clip_coef)
            sq_pair = jnp.stack([jnp.sum(weight * weight, axis=(1, 2)), jnp.sum(update * update, axis=(1, 2))])
            norm_pair = jnp.sqrt(lax.psum(sq_pair, ("model", "data")))
            trust_ratio = (norm_pair[0] / norm_pair[1])[:, None, None]
            new_weight = weight - LEARN_RATE * trust_ratio * update
            replicas.append(lax.all_gather(new_weight.astype(jnp.bfloat16), "data", axis=1, tiled=True))
            weights.append(new_weight)
            firsts.append(new_first)
            seconds.append(new_second)
        return tuple(replicas + weights + firsts + seconds)

    return jax.shard_map(device_step, mesh=mesh, in_specs=tuple(in_specs), out_specs=out_specs, check_vma=False)
```

profile of v0, /device:TPU:0, one launch (start us, length us, event | category | flops | bytes accessed | tf_op | source)
XLA Modules:
  0.0 432.5 jit_solution(11399975395122059664)
XLA Ops:
  7.2 4.2 copy.151
  11.4 5.2 %all-to-all-start.1 = ((bf16[1,2,256,1024]{3,1,0,2:T(2,128)(2,1)}), bf16[1,2,256,1024]{3,1,0,2:T(2,128)(2,1)S(1)}, u32[]{:S(2)}, u32[]{:S(2)}) async-start(bf16[1,2,256,1024]{3,1,0,2:T(2,128)(2,1)} %copy.151), calls=%async_computation.1 | async-start | bytes 2097152 | tf_op jit(solution)/shard_map/all_to_all | solution.py:50
  16.6 9.3 %copy.150 = bf16[1,2,1024,768]{3,1,0,2:T(2,128)(2,1)} copy(f32[1,2,1024,768]{3,2,1,0:T(8,128)} %param.16) | data formatting | bytes 9437184 | tf_op args[0]
  25.9 6.0 %all-to-all-done.1 = bf16[1,2,256,1024]{3,1,0,2:T(2,128)(2,1)S(1)} async-done(((bf16[1,2,256,1024]{3,1,0,2:T(2,128)(2,1)}), bf16[1,2,256,1024]{3,1,0,2:T(2,128)(2,1)S(1)}, u32[]{:S(2)}, u32[]{:S(2)}) %all-to-all-start.1) | async-done | bytes 1048608 | tf_op jit(solution)/shard_map/all_to_all | solution.py:50
  32.9 4.2 all-to-all-start
  37.1 11.9 %copy.149 = bf16[1,2,1024,1024]{3,1,0,2:T(2,128)(2,1)} copy(f32[1,2,1024,1024]{3,2,1,0:T(8,128)} %param.24) | data formatting | bytes 12582912 | tf_op args[8]
  49.0 25.9 %all-to-all-done = bf16[1,2,1024,768]{3,1,0,2:T(2,128)(2,1)S(1)} async-done(((bf16[1,2,1024,768]{3,1,0,2:T(2,128)(2,1)}), bf16[1,2,1024,768]{3,1,0,2:T(2,128)(2,1)S(1)}, u32[]{:S(2)}, u32[]{:S(2)}) %all-to-all-start) | async-done | bytes 3145760 | tf_op jit(solution)/shard_map/all_to_all | solution.py:50
  74.9 4.7 %all-to-all-start.2 = ((bf16[1,2,1024,1024]{3,1,0,2:T(2,128)(2,1)}), bf16[1,2,1024,1024]{3,1,0,2:T(2,128)(2,1)}, u32[]{:S(2)}, u32[]{:S(2)}) async-start(bf16[1,2,1024,1024]{3,1,0,2:T(2,128)(2,1)} %copy.149), calls=%async_computation.2 | async-start | bytes 8388608 | tf_op jit(solution)/shard_map/all_to_all | solution.py:50
  79.6 11.9 %copy.148 = bf16[1,2,1024,1024]{3,1,0,2:T(2,128)(2,1)} copy(f32[1,2,1024,1024]{3,2,1,0:T(8,128)} %param.28) | data formatting | bytes 12582912 | tf_op args[12]
  91.5 37.1 %all-to-all-done.2 = bf16[1,2,1024,1024]{3,1,0,2:T(2,128)(2,1)} async-done(((bf16[1,2,1024,1024]{3,1,0,2:T(2,128)(2,1)}), bf16[1,2,1024,1024]{3,1,0,2:T(2,128)(2,1)}, u32[]{:S(2)}, u32[]{:S(2)}) %all-to-all-start.2) | async-done | bytes 4194336 | tf_op jit(solution)/shard_map/all_to_all | solution.py:50
  128.6 4.6 %all-to-all-start.3 = ((bf16[1,2,1024,1024]{3,1,0,2:T(2,128)(2,1)}), bf16[1,2,1024,1024]{3,1,0,2:T(2,128)(2,1)}, u32[]{:S(2)}, u32[]{:S(2)}) async-start(bf16[1,2,1024,1024]{3,1,0,2:T(2,128)(2,1)} %copy.148), calls=%async_computation.3 | async-start | bytes 8388608 | tf_op jit(solution)/shard_map/all_to_all | solution.py:50
  133.4 2.3 convert_reduce_fusion.3
  136.5 2.7 convert_reduce_fusion.2
  142.9 6.3 %convert_reduce_fusion.1 = f32[2,128,1024]{2,0,1:T(2,128)S(1)} fusion(bf16[2,8,128,1024]{3,0,2,1:T(2,128)(2,1)} %bitcast.18), kind=kLoop, calls=%fused_computation.1 | loop fusion | flops 3932160 | bytes 5242880 | tf_op jit(solution)/shard_map/reduce_sum | solution.py:51
  150.9 31.3 %all-to-all-done.3 = bf16[1,2,1024,1024]{3,1,0,2:T(2,128)(2,1)} async-done(((bf16[1,2,1024,1024]{3,1,0,2:T(2,128)(2,1)}), bf16[1,2,1024,1024]{3,1,0,2:T(2,128)(2,1)}, u32[]{:S(2)}, u32[]{:S(2)}) %all-to-all-start.3) | async-done | bytes 4194336 | tf_op jit(solution)/shard_map/all_to_all | solution.py:50
  182.2 6.6 %convert_reduce_fusion = f32[2,128,1024]{2,0,1:T(2,128)S(1)} fusion(bf16[2,8,128,1024]{3,0,2,1:T(2,128)(2,1)} %bitcast.19), kind=kLoop, calls=%fused_computation | loop fusion | flops 3932160 | bytes 5242880 | tf_op jit(solution)/shard_map/reduce_sum | solution.py:51
  191.7 39.5 %psum.35 = f32[]{:T(128)} all-reduce(f32[]{:T(128)S(6)} %add.75), channel_id=1, replica_groups=mesh['model'=4,'data'=8] {'model','data'}, use_global_device_ids=true, to_apply=%region_9.0 | all-reduce | flops 1 | bytes 8 | tf_op jit(solution)/shard_map/psum | solution.py:53
  231.9 6.3 %multiply_reduce_fusion.1 = (f32[2]{0:T(128)S(1)}, f32[2]{0:T(128)S(1)}, f32[2,128,1024]{2,1,0:T(8,128)}, f32[2,128,1024]{2,1,0:T(8,128)}, f32[2]{0:T(128)S(1)},...) fusion(f32[2,128,1024]{2,1,0:T(8,128)S(1)} %copy-done.3, f32[]{:T(128)S(6)} %mul.245, ...), kind=kLoop, calls=%fused_computation.19 | loop fusion | flops 9437176 | bytes 12582948 | tf_op jit(solution)/shard_map/reduce_sum | solution.py:59
  239.4 1.8 multiply_reduce_fusion.8
  241.2 40.4 %all-reduce = (f32[2,2]{1,0:T(2,128)S(1)}, f32[2,2]{1,0:T(2,128)S(1)}, f32[2,2]{1,0:T(2,128)S(1)}, f32[2,2]{1,0:T(2,128)S(1)}) all-reduce(f32[2,2]{1,0:T(2,128)S(1)} %get-tuple-element.96, f32[2,2]{1,0:T(2,128)S(1)} %get-tuple-element.97, f32[2,2]{1,0:T(2,128)S(1)} %pad_maximum_fusion.2, ...), channel_id=1, replica_groups=mesh['model'=4,'data'=8] {'model','data'}, use_global_device_ids=true, to_apply=%region_11.0 | all-reduce | flops 16 | bytes 128 | tf_op jit(solution)/shard_map/psum | solution.py:60
  281.7 1.8 fusion.6
  284.4 2.7 fusion.7
  288.4 2.8 fusion.4
  292.9 3.1 fusion.5
  297.3 10.8 %all-gather.7.cloned.1.call-done = bf16[2,256,1024]{2,0,1:T(2,128)(2,1)} async-done(((bf16[2,32,1024]{2,0,1:T(2,128)(2,1)}), bf16[2,256,1024]{2,0,1:T(2,128)(2,1)}) %all-gather.7.cloned.1.call-update) | async-done | bytes 1048592 | tf_op jit(solution)/shard_map/all_gather | solution.py:63
  308.1 2.5 copy.121
  310.6 31.9 %all-gather.5.cloned.1.call-done = bf16[2,1024,768]{2,0,1:T(2,128)(2,1)} async-done(((bf16[2,128,768]{2,0,1:T(2,128)(2,1)}), bf16[2,1024,768]{2,0,1:T(2,128)(2,1)}) %all-gather.5.cloned.1.call-update) | async-done | bytes 3145744 | tf_op jit(solution)/shard_map/all_gather | solution.py:63
  342.5 4.0 copy.120
  346.5 34.8 %all-gather.11.cloned.1.call-done = bf16[2,1024,1024]{2,0,1:T(2,128)(2,1)} async-done(((bf16[2,128,1024]{2,0,1:T(2,128)(2,1)}), bf16[2,1024,1024]{2,0,1:T(2,128)(2,1)}) %all-gather.11.cloned.1.call-update) | async-done | bytes 4194320 | tf_op jit(solution)/shard_map/all_gather | solution.py:63
  381.3 5.5 %copy.123 = bf16[2,1024,1024]{2,1,0:T(8,128)(2,1)} copy(bf16[2,1024,1024]{2,0,1:T(2,128)(2,1)} %all-gather.11.cloned.1.call-done) | data formatting | bytes 8388608
  386.8 33.1 %all-gather.9.cloned.1.call-done = bf16[2,1024,1024]{2,0,1:T(2,128)(2,1)} async-done(((bf16[2,128,1024]{2,0,1:T(2,128)(2,1)}), bf16[2,1024,1024]{2,0,1:T(2,128)(2,1)}) %all-gather.9.cloned.1.call-update) | async-done | bytes 4194320 | tf_op jit(solution)/shard_map/all_gather | solution.py:63
  420.0 5.5 %copy.122 = bf16[2,1024,1024]{2,1,0:T(8,128)(2,1)} copy(bf16[2,1024,1024]{2,0,1:T(2,128)(2,1)} %all-gather.9.cloned.1.call-done) | data formatting | bytes 8388608
  (58 shorter events, 14.0 us)
Async XLA Ops:
  11.4 20.6 %all-to-all-start.1 = ((bf16[1,2,256,1024]{3,1,0,2:T(2,128)(2,1)}), bf16[1,2,256,1024]{3,1,0,2:T(2,128)(2,1)S(1)}, u32[]{:S(2)}, u32[]{:S(2)}) async-start(bf16[1,2,256,1024]{3,1,0,2:T(2,128)(2,1)} %copy.151), calls=%async_computation.1 | async-start | bytes 2097152 | tf_op jit(solution)/shard_map/all_to_all | solution.py:50
  31.9 1.0 copy-start.2
  32.9 42.0 %all-to-all-start = ((bf16[1,2,1024,768]{3,1,0,2:T(2,128)(2,1)}), bf16[1,2,1024,768]{3,1,0,2:T(2,128)(2,1)S(1)}, u32[]{:S(2)}, u32[]{:S(2)}) async-start(bf16[1,2,1024,768]{3,1,0,2:T(2,128)(2,1)} %copy.150), calls=%async_computation | async-start | bytes 6291456 | tf_op jit(solution)/shard_map/all_to_all | solution.py:50
  74.9 53.7 %all-to-all-start.2 = ((bf16[1,2,1024,1024]{3,1,0,2:T(2,128)(2,1)}), bf16[1,2,1024,1024]{3,1,0,2:T(2,128)(2,1)}, u32[]{:S(2)}, u32[]{:S(2)}) async-start(bf16[1,2,1024,1024]{3,1,0,2:T(2,128)(2,1)} %copy.149), calls=%async_computation.2 | async-start | bytes 8388608 | tf_op jit(solution)/shard_map/all_to_all | solution.py:50
  128.6 53.6 %all-to-all-start.3 = ((bf16[1,2,1024,1024]{3,1,0,2:T(2,128)(2,1)}), bf16[1,2,1024,1024]{3,1,0,2:T(2,128)(2,1)}, u32[]{:S(2)}, u32[]{:S(2)}) async-start(bf16[1,2,1024,1024]{3,1,0,2:T(2,128)(2,1)} %copy.148), calls=%async_computation.3 | async-start | bytes 8388608 | tf_op jit(solution)/shard_map/all_to_all | solution.py:50
  133.2 175.0 %all-gather.7.cloned.1.call-start = ((), (), s32[]{:S(2)}) async-start(), calls=%async_computation.5 | async-start | bytes 1179648 | tf_op jit(solution)/shard_map/all_gather | solution.py:63
  139.3 0.9 copy-start
  149.2 82.7 %copy-start.3 = (f32[2,128,1024]{2,1,0:T(8,128)S(1)}, f32[2,128,1024]{2,1,0:T(8,128)}, u32[]{:S(2)}) copy-start(f32[2,128,1024]{2,1,0:T(8,128)} %param.29) | copy-start | bytes 3145732
  231.9 6.4 %copy-start.8 = (f32[2,32,1024]{2,1,0:T(8,128)S(1)}, f32[2,32,1024]{2,1,0:T(8,128)}, u32[]{:S(2)}) copy-start(f32[2,32,1024]{2,1,0:T(8,128)} %param.21) | copy-start | bytes 786436
  231.9 6.4 %copy-start.13 = (f32[2,32,1024]{2,1,0:T(8,128)S(1)}, f32[2,32,1024]{2,1,0:T(8,128)}, u32[]{:S(2)}) copy-start(f32[2,32,1024]{2,1,0:T(8,128)} %param.22) | copy-start | bytes 786436
  231.9 6.4 %copy-start.14 = (f32[2,32,1024]{2,1,0:T(8,128)S(1)}, f32[2,32,1024]{2,1,0:T(8,128)}, u32[]{:S(2)}) copy-start(f32[2,32,1024]{2,1,0:T(8,128)} %param.23) | copy-start | bytes 786436
  231.9 7.5 %copy-start.1 = (f32[2,128,768]{2,0,1:T(2,128)S(1)}, f32[2,128,768]{2,0,1:T(2,128)}, u32[]{:S(2)}) copy-start(f32[2,128,768]{2,0,1:T(2,128)} %copy-done) | copy-start | bytes 2359300
  231.9 7.5 %copy-start.6 = (f32[2,128,768]{2,1,0:T(8,128)S(1)}, f32[2,128,768]{2,1,0:T(8,128)}, u32[]{:S(2)}) copy-start(f32[2,128,768]{2,1,0:T(8,128)} %param.17) | copy-start | bytes 2359300
  231.9 7.5 %copy-start.11 = (f32[2,128,768]{2,1,0:T(8,128)S(1)}, f32[2,128,768]{2,1,0:T(8,128)}, u32[]{:S(2)}) copy-start(f32[2,128,768]{2,1,0:T(8,128)} %param.18) | copy-start | bytes 2359300
  231.9 7.4 %copy-start.12 = (f32[2,128,768]{2,1,0:T(8,128)S(1)}, f32[2,128,768]{2,1,0:T(8,128)}, u32[]{:S(2)}) copy-start(f32[2,128,768]{2,1,0:T(8,128)} %param.19) | copy-start | bytes 2359300
  238.3 43.4 %copy-start.9 = (f32[2,32,1024]{2,1,0:T(8,128)S(1)}, f32[2,32,1024]{2,1,0:T(8,128)}, u32[]{:S(2)}) copy-start(f32[2,32,1024]{2,1,0:T(8,128)} %param.21) | copy-start | bytes 786436
  238.3 46.1 %copy-start.7 = (f32[2,128,768]{2,1,0:T(8,128)S(1)}, f32[2,128,768]{2,1,0:T(8,128)}, u32[]{:S(2)}) copy-start(f32[2,128,768]{2,1,0:T(8,128)} %param.17) | copy-start | bytes 2359300
  239.4 42.3 %copy-start.10 = (f32[2,32,1024]{2,1,0:T(8,128)S(1)}, f32[2,32,1024]{2,1,0:T(8,128)}, u32[]{:S(2)}) copy-start(f32[2,32,1024]{2,1,0:T(8,128)} %get-tuple-element.88) | copy-start | bytes 786436
  241.2 47.1 %copy-start.5 = (f32[2,128,1024]{2,1,0:T(8,128)S(1)}, f32[2,128,1024]{2,1,0:T(8,128)}, u32[]{:S(2)}) copy-start(f32[2,128,1024]{2,1,0:T(8,128)} %get-tuple-element.84) | copy-start | bytes 3145732
  284.3 58.2 %all-gather.5.cloned.1.call-start = ((), (), s32[]{:S(2)}) async-start(), calls=%async_computation.4 | async-start | bytes 3538944 | tf_op jit(solution)/shard_map/all_gather | solution.py:63
  287.1 5.8 %copy-start.4 = (f32[2,128,1024]{2,1,0:T(8,128)S(1)}, f32[2,128,1024]{2,1,0:T(8,128)}, u32[]{:S(2)}) copy-start(f32[2,128,1024]{2,1,0:T(8,128)} %param.25) | copy-start | bytes 3145732
  288.3 93.0 %all-gather.11.cloned.1.call-start = ((), (), s32[]{:S(2)}) async-start(), calls=%async_computation.7 | async-start | bytes 4718592 | tf_op jit(solution)/shard_map/all_gather | solution.py:63
  292.5 127.5 %all-gather.9.cloned.1.call-start = ((), (), s32[]{:S(2)}) async-start(), calls=%async_computation.6 | async-start | bytes 4718592 | tf_op jit(solution)/shard_map/all_gather | solution.py:63
Sparse Core Ops, SparseCore 0:
  284.4 23.6 all-gather.6
  310.6 31.8 all-gather.4
  345.0 36.2 all-gather.10
  383.6 36.2 all-gather.8
where the time goes:
time: 439 us; the launch traced here: 433 us
  waiting for transfers between devices  211 us (48%)
  blocking collectives  79.9 us (18%)
  local copies, waits for them, and re-layouts  61.2 us (14%)
  other arithmetic  43.1 us (10%)
  starting transfers between devices  19.3 us (4%)
  between operations  17.8 us (4%)
    all_gather x4, waiting for transfers between devices, device_step(): lax.all_gather(new_weight.astype(jnp.bfloat16), 'data', axis=1, tiled=True)  111 us
    all_to_all x4, waiting for transfers between devices, device_step(): received = lax.all_to_all(sent_grad, 'data', 2, 0, tiled=True)  100 us
    unnamed x38, local copies, waits for them, and re-layouts  56.6 us
    psum x1, blocking collectives, device_step(): norm_pair = jnp.sqrt(lax.psum(sq_pair, ('model', 'data')))  40.4 us
    psum x1, blocking collectives, device_step(): total_norm = jnp.sqrt(lax.psum(local_sq, ('model', 'data')))  39.5 us
    all_to_all x4, starting transfers between devices, device_step(): received = lax.all_to_all(sent_grad, 'data', 2, 0, tiled=True)  18.7 us
    reduce_sum x4, other arithmetic, device_step(): grad_means.append(jnp.sum(received, axis=0, dtype=jnp.float32) / group_size)  17.8 us
    convert_element_type x4, other arithmetic, device_step(): new_weight.astype(jnp.bfloat16)  10.4 us
  transfers between devices with their start and end apart: 8, of which 8 were waited for; matrix products, arithmetic and copies ran while one was open for 17% of the time, Pallas kernels for 0%

commit v1 on v0

v1 whole, which is shorter than its diff:
```python
import functools

import jax
import jax.numpy as jnp
from jax import lax
from jax.experimental import pallas as pl
from jax.experimental.pallas import tpu as pltpu
from jax.sharding import PartitionSpec as P

LEARN_RATE = 0.08
BETA_ONE = 0.9
BETA_TWO = 0.999
ADAM_EPS = 1e-6
DECAY_RATE = 0.01
MAX_NORM = 1.0
STEP_COUNT = 100
COLUMN_SPLIT = (True, False, True, False)

KINDS = 4
LAYERS = 2
KIND_ORDER = (1, 0, 2, 3)
ME, XN, YN, DG = 0, 1, 2, 3
MESH = pl.DeviceIdType.MESH


def grad_spec(col_split):
    return P("data", None, None, "model") if col_split else P("data", None, "model", None)


def state_spec(col_split):
    return P(None, "data", "model") if col_split else P(None, ("model", "data"), None)


def replica_spec(col_split):
    return P(None, None, "model") if col_split else P(None, "model", None)


def lane_fold(x):
    total = x[:, 0:128]
    for j in range(1, x.shape[1] // 128):
        total = total + x[:, 128 * j:128 * (j + 1)]
    return total


def kernel(n_model, n_data, dims, *refs):
    n_dev = n_model * n_data
    grads, weights, firsts, seconds = (refs[i::4][:KINDS] for i in range(4))
    grads, weights, firsts, seconds = ([refs[4 * k + i] for k in range(KINDS)] for i in range(4))
    outs = refs[16:32]
    replicas, out_w, out_m, out_v = outs[0:4], outs[4:8], outs[8:12], outs[12:16]
    scratch = refs[32:]
    acc, stage, sent, got, p1, p2, wv, mv, vv = (scratch[4 * i:4 * i + 4] for i in range(9))
    (row_a, row_b, all_a, all_b,
     ld_acc, ld_stage, ld_state, d_send, d_recv, p1_send, p1_recv, p2_send, p2_recv,
     g_send, g_recv, h_send, h_recv, st_out, rep_out, ps_send, ps_recv) = scratch[36:]

    model = lax.axis_index("model")
    data = lax.axis_index("data")
    core = data % 2
    xc = (data // 2) % 2
    yc = data // 4
    me = model * n_data + data

    def chip_of(slot):
        x = xc if slot in (ME, YN) else 1 - xc
        y = yc if slot in (ME, XN) else 1 - yc
        return 2 * y + x

    def device(slot, other_core=False):
        return (model, 2 * chip_of(slot) + ((1 - core) if other_core else core))

    partner = device(ME, True)
    to_x = device(XN)
    to_y = device(YN)

    def rows_of(k, slot, other_core):
        rows = dims[k][0]
        return pl.ds(pl.multiple_of((2 * chip_of(slot) + ((1 - core) if other_core else core)) * rows, rows), rows)

    def load_unit(l, s, k):
        return (
            pltpu.make_async_copy(grads[k].at[0, l, rows_of(k, s, True)], stage[k].at[l], ld_stage.at[k, l]),
            pltpu.make_async_copy(grads[k].at[0, l, rows_of(k, s, False)], acc[k].at[l, s], ld_acc.at[k, l, s]),
        )

    def remote(src, dst, send, recv, dev):
        return pltpu.make_async_remote_copy(src_ref=src, dst_ref=dst, send_sem=send, recv_sem=recv, device_id=dev, device_id_type=MESH)

    def pair_copy(l, s, k):
        return remote(sent[k].at[l, s], got[k].at[l, s], d_send.at[k, l, s], d_recv.at[k, l, s], partner)

    first_dev = (to_x, to_y)
    second_dev = (to_y, to_x)
    first_nb = (XN, YN)
    second_nb = (YN, XN)

    def first_copy(l, through, k):
        slot = DG if through else first_nb[l]
        t = 0 if through else 1
        return remote(acc[k].at[l, slot], p1[k].at[l, t], p1_send.at[k, l, t], p1_recv.at[k, l, t], first_dev[l])

    def second_copy(l, k):
        return remote(acc[k].at[l, second_nb[l]], p2[k].at[l], p2_send.at[k, l], p2_recv.at[k, l], second_dev[l])

    def over_rows(k, step, body):
        rows = dims[k][0]

        def run(i, carry):
            body(pl.ds(pl.multiple_of(i * step, step), step))
            return carry

        lax.fori_loop(0, rows // step, run, 0)

    def sum_rows(k, body):
        rows, cols = dims[k]
        return lane_fold(lax.fori_loop(
            0, rows // 8, lambda i, c: c + body(pl.ds(pl.multiple_of(i * 8, 8), 8)), jnp.zeros((8, cols), jnp.float32)))

    units = []
    for slots in ((DG, DG), (YN, XN), (XN, YN), (ME, ME)):
        for k in KIND_ORDER:
            for l in range(LAYERS):
                units.append((l, slots[l], k))
    ahead = 6
    for u in units[:ahead]:
        for c in load_unit(*u):
            c.start()

    barrier = pltpu.get_barrier_semaphore()

    def greet(i, carry):
        t = (me + i) % n_dev
        pl.semaphore_signal(barrier, inc=1, device_id=(t // n_data, t % n_data), device_id_type=MESH)
        return carry

    lax.fori_loop(1, n_dev, greet, 0)
    pl.semaphore_wait(barrier, n_dev - 1)

    def state_load(k):
        return [pltpu.make_async_copy(src[k], dst[k], ld_state.at[i, k]) for i, (src, dst) in enumerate(((weights, wv), (firsts, mv), (seconds, vv)))]

    def pair_half(l, s, k):
        for c in load_unit(l, s, k):
            c.wait()

        def body(r):
            sent[k][l, s, r, :] = stage[k][l, r, :].astype(jnp.bfloat16)

        over_rows(k, 16, body)
        pair_copy(l, s, k).start()

    def chip_half(l, s, k):
        pair_copy(l, s, k).wait_recv()

        def body(r):
            own = acc[k][l, s, r, :].astype(jnp.bfloat16).astype(jnp.float32)
            acc[k][l, s, r, :] = own + got[k][l, s, r, :].astype(jnp.float32)

        over_rows(k, 16, body)
        if s == DG:
            first_copy(l, True, k).start()
        elif s == first_nb[l]:
            first_copy(l, False, k).start()

    lag = 2
    for i in range(len(units) + lag):
        if i < len(units):
            pair_half(*units[i])
            if i + ahead < len(units):
                for c in load_unit(*units[i + ahead]):
                    c.start()
            elif i + ahead - len(units) < KINDS:
                for c in state_load(i + ahead - len(units)):
                    c.start()
        if i >= lag:
            chip_half(*units[i - lag])

    for k in KIND_ORDER:
        for l in range(LAYERS):
            first_copy(l, True, k).wait_recv()
            s = second_nb[l]

            def body(r):
                acc[k][l, s, r, :] = acc[k][l, s, r, :] + p1[k][l, 0, r, :]

            over_rows(k, 8, body)
            second_copy(l, k).start()

    lane = lax.broadcasted_iota(jnp.int32, (1, 128), 1)
    norms = jnp.zeros((1, 128), jnp.float32)
    for k in range(KINDS):
        for c in state_load(k):
            c.wait()
        for l in range(LAYERS):
            part = sum_rows(k, lambda r: wv[k][l, r, :] * wv[k][l, r, :])
            norms = norms + jnp.where(lane == 2 * k + l, jnp.sum(part, keepdims=True), 0.0)

    for k in KIND_ORDER:
        for l in range(LAYERS):
            first_copy(l, False, k).wait_recv()

            def body(r):
                acc[k][l, ME, r, :] = acc[k][l, ME, r, :] + p1[k][l, 1, r, :]

            over_rows(k, 8, body)

    grad_sq = jnp.zeros((8, 128), jnp.float32)
    for k in KIND_ORDER:
        for l in range(LAYERS):
            second_copy(l, k).wait_recv()

            def body(r):
                mean = (acc[k][l, ME, r, :] + p2[k][l, r, :]) * (1.0 / n_data)
                acc[k][l, ME, r, :] = mean
                return mean * mean

            grad_sq = grad_sq + sum_rows(k, body)
    norms = norms + jnp.where(lane == 8, jnp.sum(grad_sq, keepdims=True), 0.0)

    def exchange(which, row_ref, all_ref, row):
        row_ref[...] = row
        all_ref[me] = row

        def send(i, carry):
            t = (me + i) % n_dev
            remote(row_ref, all_ref.at[me], ps_send.at[which], ps_recv.at[which], (t // n_data, t % n_data)).start()
            return carry

        lax.fori_loop(1, n_dev, send, 0)
        rest = all_ref.at[pl.ds(0, n_dev - 1)]
        pltpu.make_async_copy(rest, rest, ps_recv.at[which]).wait()
        return jnp.sum(all_ref[...], axis=0)

    norms = exchange(0, row_a, all_a, norms)

    def pick(row, i):
        return jnp.sum(jnp.where(lane == i, row, 0.0), axis=1, keepdims=True)

    clip = jnp.minimum(1.0, MAX_NORM / jnp.sqrt(pick(norms, 8)))

    squares = jnp.zeros((1, 128), jnp.float32)
    for k in KIND_ORDER:
        for l in range(LAYERS):

            def body(r):
                clipped = clip * acc[k][l, ME, r, :]
                weight = wv[k][l, r, :]
                first = BETA_ONE * mv[k][l, r, :] + (1.0 - BETA_ONE) * clipped
                second = BETA_TWO * vv[k][l, r, :] + (1.0 - BETA_TWO) * clipped * clipped
                mv[k][l, r, :] = first
                vv[k][l, r, :] = second
                first_hat = first * (1.0 / (1.0 - BETA_ONE ** STEP_COUNT))
                second_hat = second * (1.0 / (1.0 - BETA_TWO ** STEP_COUNT))
                update = first_hat / (jnp.sqrt(second_hat) + ADAM_EPS) + DECAY_RATE * weight
                acc[k][l, ME, r, :] = update
                return update * update

            part = sum_rows(k, body)
            squares = squares + jnp.where(lane == 2 * k + l, jnp.sum(part, keepdims=True), 0.0)

    for (l, s, k) in units:
        pair_copy(l, s, k).wait_send()
    for k in range(KINDS):
        for l in range(LAYERS):
            first_copy(l, True, k).wait_send()
            first_copy(l, False, k).wait_send()
            second_copy(l, k).wait_send()

    squares = exchange(1, row_b, all_b, squares)
    for k in range(KINDS):
        pltpu.make_async_copy(mv[k], out_m[k], st_out.at[1, k]).start()
        pltpu.make_async_copy(vv[k], out_v[k], st_out.at[2, k]).start()
    ratios = jnp.sqrt(norms) / jnp.sqrt(squares)

    def own_copy(l, along, k):
        return remote(sent[k].at[l, ME], sent[k].at[l, along], g_send.at[k, l, along], g_recv.at[k, l, along], to_x if along == XN else to_y)

    def pass_copy(l, k):
        return remote(sent[k].at[l, first_nb[l]], sent[k].at[l, DG], g_send.at[k, l, DG], g_recv.at[k, l, DG], second_dev[l])

    def half_copy(l, s, k):
        return remote(sent[k].at[l, s], got[k].at[l, s], h_send.at[k, l, s], h_recv.at[k, l, s], partner)

    def write(l, s, k, other_core):
        src = got if other_core else sent
        pltpu.make_async_copy(src[k].at[l, s], replicas[k].at[l, rows_of(k, s, other_core)], rep_out.at[k]).start()

    pending = []

    def spread(l, s, k):
        half_copy(l, s, k).start()
        write(l, s, k, False)
        pending.append((l, s, k))

    def collect(keep):
        while len(pending) > keep:
            l, s, k = pending.pop(0)
            half_copy(l, s, k).wait_recv()
            write(l, s, k, True)

    for k in KIND_ORDER:
        for l in range(LAYERS):
            scale = LEARN_RATE * pick(ratios, 2 * k + l)

            def body(r):
                fresh = wv[k][l, r, :] - scale * acc[k][l, ME, r, :]
                wv[k][l, r, :] = fresh
                sent[k][l, ME, r, :] = fresh.astype(jnp.bfloat16)

            over_rows(k, 16, body)
            own_copy(l, first_nb[l], k).start()
    for k in KIND_ORDER:
        for l in range(LAYERS):
            own_copy(l, second_nb[l], k).start()
            spread(l, ME, k)
        pltpu.make_async_copy(wv[k], out_w[k], st_out.at[0, k]).start()

    for k in KIND_ORDER:
        for l in range(LAYERS):
            own_copy(l, first_nb[l], k).wait_recv()
            pass_copy(l, k).start()
            spread(l, first_nb[l], k)
            collect(2)
    for k in KIND_ORDER:
        for l in range(LAYERS):
            own_copy(l, second_nb[l], k).wait_recv()
            spread(l, second_nb[l], k)
            collect(2)
    for k in KIND_ORDER:
        for l in range(LAYERS):
            pass_copy(l, k).wait_recv()
            spread(l, DG, k)
            collect(2)
    collect(0)

    for k in range(KINDS):
        for l in range(LAYERS):
            own_copy(l, XN, k).wait_send()
            own_copy(l, YN, k).wait_send()
            pass_copy(l, k).wait_send()
            for s in range(4):
                half_copy(l, s, k).wait_send()
    for which, all_ref in ((0, all_a), (1, all_b)):
        rest = all_ref.at[pl.ds(0, n_dev - 1)]
        pltpu.make_async_copy(rest, rest, ps_send.at[which]).wait()
    for k in range(KINDS):
        pltpu.make_async_copy(replicas[k], replicas[k], rep_out.at[k]).wait()
        pltpu.make_async_copy(wv[k], out_w[k], st_out.at[0, k]).wait()
        pltpu.make_async_copy(mv[k], out_m[k], st_out.at[1, k]).wait()
        pltpu.make_async_copy(vv[k], out_v[k], st_out.at[2, k]).wait()


def solution(mesh):
    n_model, n_data = mesh.shape["model"], mesh.shape["data"]
    in_specs = []
    for col_split in COLUMN_SPLIT:
        in_specs.extend([grad_spec(col_split), state_spec(col_split), state_spec(col_split), state_spec(col_split)])
    out_specs = tuple([replica_spec(col_split) for col_split in COLUMN_SPLIT] + [state_spec(col_split) for col_split in COLUMN_SPLIT] * 3)

    def device_step(*arrays):
        dims = [arrays[4 * k + 1].shape[1:] for k in range(KINDS)]
        f32, bf16 = jnp.float32, jnp.bfloat16
        out_shape = [jax.ShapeDtypeStruct((LAYERS, n_data * d[0], d[1]), bf16) for d in dims]
        out_shape += [jax.ShapeDtypeStruct((LAYERS,) + tuple(d), f32) for d in dims] * 3

        def each(prefix, dtype):
            return [pltpu.VMEM(prefix + tuple(d), dtype) for d in dims]

        dma = pltpu.SemaphoreType.DMA
        n_dev = n_model * n_data
        scratch = (each((LAYERS, 4), f32) + each((LAYERS,), f32) + each((LAYERS, 4), bf16) + each((LAYERS, 4), bf16)
                   + each((LAYERS, 2), f32) + each((LAYERS,), f32) + each((LAYERS,), f32) * 3)
        scratch += [pltpu.VMEM((1, 128), f32), pltpu.VMEM((1, 128), f32), pltpu.VMEM((n_dev, 1, 128), f32), pltpu.VMEM((n_dev, 1, 128), f32)]
        scratch += [dma((4, 2, 4)), dma((4, 2)), dma((3, 4)), dma((4, 2, 4)), dma((4, 2, 4)), dma((4, 2, 2)), dma((4, 2, 2)), dma((4, 2)), dma((4, 2)),
                    dma((4, 2, 4)), dma((4, 2, 4)), dma((4, 2, 4)), dma((4, 2, 4)), dma((3, 4)), dma((4,)), dma((2,)), dma((2,))]
        return tuple(pl.pallas_call(
            functools.partial(kernel, n_model, n_data, dims),
            out_shape=out_shape,
            in_specs=[pl.BlockSpec(memory_space=pl.ANY)] * 16,
            out_specs=[pl.BlockSpec(memory_space=pl.ANY)] * 16,
            scratch_shapes=scratch,
            compiler_params=pltpu.CompilerParams(collective_id=0, has_side_effects=True, vmem_limit_bytes=60 * 1024 * 1024),
            name="lamb_step",
        )(*arrays))

    return jax.shard_map(device_step, mesh=mesh, in_specs=tuple(in_specs), out_specs=out_specs, check_vma=False)
```

time: 439 us -> 206 us (0.47); the launches traced: 433 us -> 205 us
  waiting for transfers between devices: 211 us -> 0 us
  Pallas kernels: 0 us -> 183 us
  blocking collectives: 79.9 us -> 0 us
  other arithmetic: 43.1 us -> 0 us
  local copies, waits for them, and re-layouts: 61.2 us -> 21.3 us
  starting transfers between devices: 19.3 us -> 0 us
  between operations: 17.8 us -> 0.71 us
    pallas_call x0 -> x1, Pallas kernels: none -> 183 us  [device_step(): pl.pallas_call(functools.partial(kernel, n_model, n_data, dims), out_shap...]
    all_gather x4 -> x0, waiting for transfers between devices: 111 us -> none  [device_step(): lax.all_gather(new_weight.astype(jnp.bfloat16), 'data', axis=1, tiled=True)]
    all_to_all x4 -> x0, waiting for transfers between devices: 100 us -> none  [device_step(): received = lax.all_to_all(sent_grad, 'data', 2, 0, tiled=True)]
    psum x2 -> x0, blocking collectives: 79.9 us -> none  [the longest x1 40.4 us: device_step(): norm_pair = jnp.sqrt(lax.psum(sq_pair, ('model', 'data')))]
    unnamed x38 -> x46, local copies, waits for them, and re-layouts: 56.6 us -> 21.3 us
    reduce_sum x11 -> x0, other arithmetic: 32.6 us -> none  [the longest x4 17.8 us: device_step(): grad_means.append(jnp.sum(received, axis=0, dtype=jnp.float32) / group_size)]
    all_to_all x4 -> x0, starting transfers between devices: 18.7 us -> none  [device_step(): received = lax.all_to_all(sent_grad, 'data', 2, 0, tiled=True)]
    convert_element_type x4 -> x0, other arithmetic: 10.4 us -> none  [device_step(): new_weight.astype(jnp.bfloat16)]
  transfers between devices with their start and end apart: 8 -> 0, of which waited for: 8 -> 0; matrix products, arithmetic and copies ran while one was open for 17% -> 0% of each run, Pallas kernels for 0% -> 0%
where the time goes in v1:
time: 206 us; the launch traced here: 205 us
  Pallas kernels  183 us (89%)
  local copies, waits for them, and re-layouts  21.3 us (10%)
    pallas_call x1, Pallas kernels, device_step(): pl.pallas_call(functools.partial(kernel, n_model, n_data, dims), out_shap...  183 us
    unnamed x46, local copies, waits for them, and re-layouts  21.3 us

profile of v1, /device:TPU:0, one launch (start us, length us, event | category | flops | bytes accessed | tf_op | source)
XLA Modules:
  0.0 204.9 jit_solution(14095755901485431517)
XLA Ops:
  0.7 182.9 %lamb_step.1 = (bf16[2,1024,768]{2,1,0:T(8,128)(2,1)}, bf16[2,256,1024]{2,1,0:T(8,128)(2,1)}, bf16[2,1024,1024]{2,1,0:T(8,128)(2,1)}, bf16[2,1024,1024]{2,1,0:T(...) custom-call(f32[1,2,1024,768]{3,2,1,0:T(8,128)} %refs_0_.1, ...), custom_call_target="tpu_custom_call" | custom-call | tf_op jit(solution)/shard_map/lamb_step/pallas_call | solution.py:376
  183.6 0.0 copy-start.8
  183.6 0.0 copy-start.1
  183.6 3.9 %copy.48 = bf16[2,1024,768]{2,1,0:T(8,128)(2,1)} copy(bf16[2,1024,768]{2,1,0:T(8,128)(2,1)} %get-tuple-element.32) | data formatting | bytes 6291456
  187.5 0.0 copy-done.8
  187.5 1.0 copy.49
  188.5 0.0 copy-done.1
  188.5 2.1 %copy.50 = bf16[2,1024,1024]{2,1,0:T(8,128)(2,1)} copy(bf16[2,1024,1024]{2,1,0:T(8,128)(2,1)S(1)} %copy-done.1) | data formatting | bytes 8388608
  190.6 1.6 copy-done
  192.2 2.1 %copy.51 = bf16[2,1024,1024]{2,1,0:T(8,128)(2,1)} copy(bf16[2,1024,1024]{2,1,0:T(8,128)(2,1)S(1)} %copy-done) | data formatting | bytes 8388608
  194.3 0.0 copy-done.11
  194.3 0.0 copy-start.5
  194.3 0.9 copy.52
  195.2 0.0 copy-done.14
  195.2 0.7 copy.53
  195.9 0.0 copy-done.7
  195.9 1.0 copy.54
  196.9 0.0 copy-done.6
  196.9 1.0 copy.55
  197.9 0.0 copy-done.10
  197.9 0.9 copy.56
  198.8 0.0 copy-done.13
  198.8 0.7 copy.57
  199.5 0.0 copy-done.5
  199.5 1.0 copy.58
  200.4 0.0 copy-done.4
  200.4 1.0 copy.59
  201.4 0.9 copy.60
  202.3 0.0 copy-done.12
  202.3 0.7 copy.61
  203.0 1.0 copy.62
  204.0 1.0 copy.63
  (15 shorter events, 0.0 us)
Async XLA Ops:
  183.6 3.9 %copy-start.8 = (bf16[2,256,1024]{2,1,0:T(8,128)(2,1)S(1)}, bf16[2,256,1024]{2,1,0:T(8,128)(2,1)}, u32[]{:S(2)}) copy-start(bf16[2,256,1024]{2,1,0:T(8,128)(2,1)} %get-tuple-element.33) | copy-start | bytes 3145732
  183.6 4.9 %copy-start.1 = (bf16[2,1024,1024]{2,1,0:T(8,128)(2,1)S(1)}, bf16[2,1024,1024]{2,1,0:T(8,128)(2,1)}, u32[]{:S(2)}) copy-start(bf16[2,1024,1024]{2,1,0:T(8,128)(2,1)} %get-tuple-element.34) | copy-start | bytes 12582916
  188.5 3.7 %copy-start = (bf16[2,1024,1024]{2,1,0:T(8,128)(2,1)S(1)}, bf16[2,1024,1024]{2,1,0:T(8,128)(2,1)}, u32[]{:S(2)}) copy-start(bf16[2,1024,1024]{2,1,0:T(8,128)(2,1)} %get-tuple-element.35) | copy-start | bytes 12582916
  192.2 2.1 %copy-start.11 = (f32[2,128,768]{2,1,0:T(8,128)S(1)}, f32[2,128,768]{2,1,0:T(8,128)}, u32[]{:S(2)}) copy-start(f32[2,128,768]{2,1,0:T(8,128)} %get-tuple-element.36) | copy-start | bytes 2359300
  192.2 3.0 %copy-start.14 = (f32[2,32,1024]{2,1,0:T(8,128)S(1)}, f32[2,32,1024]{2,1,0:T(8,128)}, u32[]{:S(2)}) copy-start(f32[2,32,1024]{2,1,0:T(8,128)} %get-tuple-element.37) | copy-start | bytes 786436
  192.2 3.7 %copy-start.7 = (f32[2,128,1024]{2,1,0:T(8,128)S(1)}, f32[2,128,1024]{2,1,0:T(8,128)}, u32[]{:S(2)}) copy-start(f32[2,128,1024]{2,1,0:T(8,128)} %get-tuple-element.38) | copy-start | bytes 3145732
  194.3 2.6 %copy-start.6 = (f32[2,128,1024]{2,1,0:T(8,128)S(1)}, f32[2,128,1024]{2,1,0:T(8,128)}, u32[]{:S(2)}) copy-start(f32[2,128,1024]{2,1,0:T(8,128)} %get-tuple-element.39) | copy-start | bytes 3145732
  194.3 3.6 %copy-start.10 = (f32[2,128,768]{2,1,0:T(8,128)S(1)}, f32[2,128,768]{2,1,0:T(8,128)}, u32[]{:S(2)}) copy-start(f32[2,128,768]{2,1,0:T(8,128)} %get-tuple-element.40) | copy-start | bytes 2359300
  194.3 4.4 %copy-start.13 = (f32[2,32,1024]{2,1,0:T(8,128)S(1)}, f32[2,32,1024]{2,1,0:T(8,128)}, u32[]{:S(2)}) copy-start(f32[2,32,1024]{2,1,0:T(8,128)} %get-tuple-element.41) | copy-start | bytes 786436
  194.3 5.1 %copy-start.5 = (f32[2,128,1024]{2,1,0:T(8,128)S(1)}, f32[2,128,1024]{2,1,0:T(8,128)}, u32[]{:S(2)}) copy-start(f32[2,128,1024]{2,1,0:T(8,128)} %get-tuple-element.42) | copy-start | bytes 3145732
  195.9 4.5 %copy-start.4 = (f32[2,128,1024]{2,1,0:T(8,128)S(1)}, f32[2,128,1024]{2,1,0:T(8,128)}, u32[]{:S(2)}) copy-start(f32[2,128,1024]{2,1,0:T(8,128)} %get-tuple-element.43) | copy-start | bytes 3145732
  196.9 4.5 %copy-start.9 = (f32[2,128,768]{2,1,0:T(8,128)S(1)}, f32[2,128,768]{2,1,0:T(8,128)}, u32[]{:S(2)}) copy-start(f32[2,128,768]{2,1,0:T(8,128)} %get-tuple-element.44) | copy-start | bytes 2359300
  197.9 4.4 %copy-start.12 = (f32[2,32,1024]{2,1,0:T(8,128)S(1)}, f32[2,32,1024]{2,1,0:T(8,128)}, u32[]{:S(2)}) copy-start(f32[2,32,1024]{2,1,0:T(8,128)} %get-tuple-element.45) | copy-start | bytes 786436
  197.9 5.1 %copy-start.3 = (f32[2,128,1024]{2,1,0:T(8,128)S(1)}, f32[2,128,1024]{2,1,0:T(8,128)}, u32[]{:S(2)}) copy-start(f32[2,128,1024]{2,1,0:T(8,128)} %get-tuple-element.46) | copy-start | bytes 3145732
  199.5 4.5 %copy-start.2 = (f32[2,128,1024]{2,1,0:T(8,128)S(1)}, f32[2,128,1024]{2,1,0:T(8,128)}, u32[]{:S(2)}) copy-start(f32[2,128,1024]{2,1,0:T(8,128)} %get-tuple-element.47) | copy-start | bytes 3145732

commit v2 on v1

--- a/solution.py
+++ b/solution.py
@@ -21,6 +21,7 @@
 KIND_ORDER = (1, 0, 2, 3)
 ME, XN, YN, DG = 0, 1, 2, 3
 MESH = pl.DeviceIdType.MESH
+COMM_VMEM = 42 << 20
 
 
 def grad_spec(col_split):
@@ -44,15 +45,14 @@
 
 def kernel(n_model, n_data, dims, *refs):
     n_dev = n_model * n_data
-    grads, weights, firsts, seconds = (refs[i::4][:KINDS] for i in range(4))
     grads, weights, firsts, seconds = ([refs[4 * k + i] for k in range(KINDS)] for i in range(4))
     outs = refs[16:32]
-    replicas, out_w, out_m, out_v = outs[0:4], outs[4:8], outs[8:12], outs[12:16]
+    replicas, wv, mv, vv = outs[0:4], outs[4:8], outs[8:12], outs[12:16]
     scratch = refs[32:]
-    acc, stage, sent, got, p1, p2, wv, mv, vv = (scratch[4 * i:4 * i + 4] for i in range(9))
+    acc, stage, sent, got, p1, p2 = (scratch[4 * i:4 * i + 4] for i in range(6))
     (row_a, row_b, all_a, all_b,
      ld_acc, ld_stage, ld_state, d_send, d_recv, p1_send, p1_recv, p2_send, p2_recv,
-     g_send, g_recv, h_send, h_recv, st_out, rep_out, ps_send, ps_recv) = scratch[36:]
+     g_send, g_recv, h_send, h_recv, ps_send, ps_recv) = scratch[24:]
 
     model = lax.axis_index("model")
     data = lax.axis_index("data")
@@ -258,6 +258,53 @@
             part = sum_rows(k, body)
             squares = squares + jnp.where(lane == 2 * k + l, jnp.sum(part, keepdims=True), 0.0)
 
+    squares = exchange(1, row_b, all_b, squares)
+    ratios = jnp.sqrt(norms) / jnp.sqrt(squares)
+
+    def block(l, s, k):
+        return replicas[k].at[l, rows_of(k, s, False)]
+
+    def own_copy(l, along, k):
+        return remote(block(l, ME, k), block(l, ME, k), g_send.at[k, l, along], g_recv.at[k, l, along], to_x if along == XN else to_y)
+
+    def pass_copy(l, k):
+        src = block(l, first_nb[l], k)
+        return remote(src, src, g_send.at[k, l, DG], g_recv.at[k, l, DG], second_dev[l])
+
+    def half_copy(l, s, k):
+        return remote(block(l, s, k), block(l, s, k), h_send.at[k, l, s], h_recv.at[k, l, s], partner)
+
+    for k in KIND_ORDER:
+        for l in range(LAYERS):
+            scale = LEARN_RATE * pick(ratios, 2 * k + l)
+            start = pl.multiple_of(data * dims[k][0], dims[k][0])
+
+            def body(r, at):
+                fresh = wv[k][l, r, :] - scale * acc[k][l, ME, r, :]
+                wv[k][l, r, :] = fresh
+                replicas[k][l, pl.ds(pl.multiple_of(start + at, 16), 16), :] = fresh.astype(jnp.bfloat16)
+
+            lax.fori_loop(0, dims[k][0] // 16, lambda i, c: (body(pl.ds(pl.multiple_of(i * 16, 16), 16), i * 16), c)[1], 0)
+            own_copy(l, first_nb[l], k).start()
+    for k in KIND_ORDER:
+        for l in range(LAYERS):
+            own_copy(l, second_nb[l], k).start()
+            half_copy(l, ME, k).start()
+
+    for k in KIND_ORDER:
+        for l in range(LAYERS):
+            own_copy(l, first_nb[l], k).wait_recv()
+            pass_copy(l, k).start()
+            half_copy(l, first_nb[l], k).start()
+    for k in KIND_ORDER:
+        for l in range(LAYERS):
+            own_copy(l, second_nb[l], k).wait_recv()
+            half_copy(l, second_nb[l], k).start()
+    for k in KIND_ORDER:
+        for l in range(LAYERS):
+            pass_copy(l, k).wait_recv()
+            half_copy(l, DG, k).start()
+
     for (l, s, k) in units:
         pair_copy(l, s, k).wait_send()
     for k in range(KINDS):
@@ -265,73 +312,6 @@
             first_copy(l, True, k).wait_send()
             first_copy(l, False, k).wait_send()
             second_copy(l, k).wait_send()
-
-    squares = exchange(1, row_b, all_b, squares)
-    for k in range(KINDS):
-        pltpu.make_async_copy(mv[k], out_m[k], st_out.at[1, k]).start()
-        pltpu.make_async_copy(vv[k], out_v[k], st_out.at[2, k]).start()
-    ratios = jnp.sqrt(norms) / jnp.sqrt(squares)
-
-    def own_copy(l, along, k):
-        return remote(sent[k].at[l, ME], sent[k].at[l, along], g_send.at[k, l, along], g_recv.at[k, l, along], to_x if along == XN else to_y)
-
-    def pass_copy(l, k):
-        return remote(sent[k].at[l, first_nb[l]], sent[k].at[l, DG], g_send.at[k, l, DG], g_recv.at[k, l, DG], second_dev[l])
-
-    def half_copy(l, s, k):
-        return remote(sent[k].at[l, s], got[k].at[l, s], h_send.at[k, l, s], h_recv.at[k, l, s], partner)
-
-    def write(l, s, k, other_core):
-        src = got if other_core else sent
-        pltpu.make_async_copy(src[k].at[l, s], replicas[k].at[l, rows_of(k, s, other_core)], rep_out.at[k]).start()
-
-    pending = []
-
-    def spread(l, s, k):
-        half_copy(l, s, k).start()
-        write(l, s, k, False)
-        pending.append((l, s, k))
-
-    def collect(keep):
-        while len(pending) > keep:
-            l, s, k = pending.pop(0)
-            half_copy(l, s, k).wait_recv()
-            write(l, s, k, True)
-
-    for k in KIND_ORDER:
-        for l in range(LAYERS):
-            scale = LEARN_RATE * pick(ratios, 2 * k + l)
-
-            def body(r):
-                fresh = wv[k][l, r, :] - scale * acc[k][l, ME, r, :]
-                wv[k][l, r, :] = fresh
-                sent[k][l, ME, r, :] = fresh.astype(jnp.bfloat16)
-
-            over_rows(k, 16, body)
-            own_copy(l, first_nb[l], k).start()
-    for k in KIND_ORDER:
-        for l in range(LAYERS):
-            own_copy(l, second_nb[l], k).start()
-            spread(l, ME, k)
-        pltpu.make_async_copy(wv[k], out_w[k], st_out.at[0, k]).start()
-
-    for k in KIND_ORDER:
-        for l in range(LAYERS):
-            own_copy(l, first_nb[l], k).wait_recv()
-            pass_copy(l, k).start()
-            spread(l, first_nb[l], k)
-            collect(2)
-    for k in KIND_ORDER:
-        for l in range(LAYERS):
-            own_copy(l, second_nb[l], k).wait_recv()
-            spread(l, second_nb[l], k)
-            collect(2)
-    for k in KIND_ORDER:
-        for l in range(LAYERS):
-            pass_copy(l, k).wait_recv()
-            spread(l, DG, k)
-            collect(2)
-    collect(0)
 
     for k in range(KINDS):
         for l in range(LAYERS):
@@ -339,15 +319,18 @@
             own_copy(l, YN, k).wait_send()
             pass_copy(l, k).wait_send()
             for s in range(4):
-                half_copy(l, s, k).wait_send()
+                half_copy(l, s, k).wait()
     for which, all_ref in ((0, all_a), (1, all_b)):
         rest = all_ref.at[pl.ds(0, n_dev - 1)]
         pltpu.make_async_copy(rest, rest, ps_send.at[which]).wait()
-    for k in range(KINDS):
-        pltpu.make_async_copy(replicas[k], replicas[k], rep_out.at[k]).wait()
-        pltpu.make_async_copy(wv[k], out_w[k], st_out.at[0, k]).wait()
-        pltpu.make_async_copy(mv[k], out_m[k], st_out.at[1, k]).wait()
-        pltpu.make_async_copy(vv[k], out_v[k], st_out.at[2, k]).wait()
+
+def write_out(count, *refs):
+    srcs, dsts, sems = refs[:count], refs[count:2 * count], refs[2 * count]
+    copies = [pltpu.make_async_copy(src, dst, sems.at[i]) for i, (src, dst) in enumerate(zip(srcs, dsts))]
+    for c in copies:
+        c.start()
+    for c in copies:
+        c.wait()
 
 
 def solution(mesh):
@@ -369,18 +352,28 @@
         dma = pltpu.SemaphoreType.DMA
         n_dev = n_model * n_data
         scratch = (each((LAYERS, 4), f32) + each((LAYERS,), f32) + each((LAYERS, 4), bf16) + each((LAYERS, 4), bf16)
-                   + each((LAYERS, 2), f32) + each((LAYERS,), f32) + each((LAYERS,), f32) * 3)
+                   + each((LAYERS, 2), f32) + each((LAYERS,), f32))
         scratch += [pltpu.VMEM((1, 128), f32), pltpu.VMEM((1, 128), f32), pltpu.VMEM((n_dev, 1, 128), f32), pltpu.VMEM((n_dev, 1, 128), f32)]
         scratch += [dma((4, 2, 4)), dma((4, 2)), dma((3, 4)), dma((4, 2, 4)), dma((4, 2, 4)), dma((4, 2, 2)), dma((4, 2, 2)), dma((4, 2)), dma((4, 2)),
-                    dma((4, 2, 4)), dma((4, 2, 4)), dma((4, 2, 4)), dma((4, 2, 4)), dma((3, 4)), dma((4,)), dma((2,)), dma((2,))]
+                    dma((4, 2, 4)), dma((4, 2, 4)), dma((4, 2, 4)), dma((4, 2, 4)), dma((2,)), dma((2,))]
+        held = pl.pallas_call(
+            functools.partial(kernel, n_model, n_data, dims),
+            out_shape=[pltpu.VMEM(o.shape, o.dtype) for o in out_shape],
+            in_specs=[pl.BlockSpec(memory_space=pl.ANY)] * 16,
+            out_specs=[pl.BlockSpec(memory_space=pltpu.VMEM)] * 16,
+            scratch_shapes=scratch,
+            compiler_params=pltpu.CompilerParams(collective_id=0, has_side_effects=True, vmem_limit_bytes=COMM_VMEM),
+            name="lamb_step",
+        )(*arrays)
+        held = [pltpu.with_memory_space_constraint(h, pltpu.VMEM) for h in held]
         return tuple(pl.pallas_call(
-            functools.partial(kernel, n_model, n_data, dims),
+            functools.partial(write_out, len(out_shape)),
             out_shape=out_shape,
-            in_specs=[pl.BlockSpec(memory_space=pl.ANY)] * 16,
+            in_specs=[pl.BlockSpec(memory_space=pltpu.VMEM)] * 16,
             out_specs=[pl.BlockSpec(memory_space=pl.ANY)] * 16,
-            scratch_shapes=scratch,
-            compiler_params=pltpu.CompilerParams(collective_id=0, has_side_effects=True, vmem_limit_bytes=60 * 1024 * 1024),
-            name="lamb_step",
-        )(*arrays))
+            scratch_shapes=[dma((16,))],
+            compiler_params=pltpu.CompilerParams(vmem_limit_bytes=1 << 20),
+            name="write_out",
+        )(*held))
 
     return jax.shard_map(device_step, mesh=mesh, in_specs=tuple(in_specs), out_specs=out_specs, check_vma=False)

time: 206 us -> 191 us (0.927)
  local copies, waits for them, and re-layouts: 21.3 us -> 0 us
  Pallas kernels: 183 us -> 190 us
    unnamed x46 -> x0, local copies, waits for them, and re-layouts: 21.3 us -> none
    pallas_call x0 -> x1, Pallas kernels: none -> 7.56 us  [device_step(): pl.pallas_call(functools.partial(write_out, len(out_shape)), out_shape=ou...]
where the time goes in v2:
time: 191 us
  Pallas kernels  190 us (99%)
    pallas_call x1, Pallas kernels, device_step(): pl.pallas_call(functools.partial(kernel, n_model, n_data, dims), out_shap...  183 us
    pallas_call x1, Pallas kernels, device_step(): pl.pallas_call(functools.partial(write_out, len(out_shape)), out_shape=ou...  7.56 us

profile of v2, /device:TPU:0, one launch (start us, length us, event | category | flops | bytes accessed | tf_op | source)
XLA Modules:
  0.0 191.0 jit_solution(3297125431311911565)
XLA Ops:
  0.7 182.7 %lamb_step.1 = (bf16[2,1024,768]{2,1,0:T(8,128)(2,1)S(1)}, bf16[2,256,1024]{2,1,0:T(8,128)(2,1)S(1)}, bf16[2,1024,1024]{2,1,0:T(8,128)(2,1)S(1)}, bf16[2,1024,10...) custom-call(f32[1,2,1024,768]{3,2,1,0:T(8,128)} %refs_0_.1, ...), custom_call_target="tpu_custom_call" | custom-call | tf_op jit(solution)/shard_map/lamb_step/pallas_call | solution.py:359
  183.4 7.6 %write_out.1 = (bf16[2,1024,768]{2,1,0:T(8,128)(2,1)}, bf16[2,256,1024]{2,1,0:T(8,128)(2,1)}, bf16[2,1024,1024]{2,1,0:T(8,128)(2,1)}, bf16[2,1024,1024]{2,1,0:T(...) custom-call(bf16[2,1024,768]{2,1,0:T(8,128)(2,1)S(1)} %get-tuple-ele, ...), custom_call_target="tpu_custom_call" | custom-call | tf_op jit(solution)/shard_map/write_out/pallas_call | solution.py:369

commit v3 on v2

v3 whole, which is shorter than its diff:
```python
import functools

import jax
import jax.numpy as jnp
from jax import lax
from jax.experimental import pallas as pl
from jax.experimental.pallas import tpu as pltpu
from jax.sharding import PartitionSpec as P

LEARN_RATE = 0.08
BETA_ONE = 0.9
BETA_TWO = 0.999
ADAM_EPS = 1e-6
DECAY_RATE = 0.01
MAX_NORM = 1.0
STEP_COUNT = 100
COLUMN_SPLIT = (True, False, True, False)

KINDS = 4
LAYERS = 2
KIND_ORDER = (1, 0, 2, 3)
ME, XN, YN, DG = 0, 1, 2, 3
MESH = pl.DeviceIdType.MESH
COMM_VMEM = 42 << 20


def grad_spec(col_split):
    return P("data", None, None, "model") if col_split else P("data", None, "model", None)


def state_spec(col_split):
    return P(None, "data", "model") if col_split else P(None, ("model", "data"), None)


def replica_spec(col_split):
    return P(None, None, "model") if col_split else P(None, "model", None)


def lane_fold(x):
    total = x[:, 0:128]
    for j in range(1, x.shape[1] // 128):
        total = total + x[:, 128 * j:128 * (j + 1)]
    return total


def kernel(n_model, n_data, dims, *refs):
    n_dev = n_model * n_data
    grads, weights, firsts, seconds = ([refs[4 * k + i] for k in range(KINDS)] for i in range(4))
    outs = refs[16:32]
    replicas, wv, mv, vv = outs[0:4], outs[4:8], outs[8:12], outs[12:16]
    scratch = refs[32:]
    acc, stage, sent, got, p1, p2 = (scratch[4 * i:4 * i + 4] for i in range(6))
    (row_ref, all_ref, ld_unit, ld_state, d_send, d_recv, p1_send, p1_recv, p2_send, p2_recv,
     g_send, g_recv, h_send, h_recv, ps_send, ps_recv, rounds) = scratch[24:]

    model = lax.axis_index("model")
    data = lax.axis_index("data")
    core = data % 2
    xc = (data // 2) % 2
    yc = data // 4
    me = model * n_data + data

    def chip_of(slot):
        x = xc if slot in (ME, YN) else 1 - xc
        y = yc if slot in (ME, XN) else 1 - yc
        return 2 * y + x

    def device(slot, other_core=False):
        return (model, 2 * chip_of(slot) + ((1 - core) if other_core else core))

    partner = device(ME, True)
    to_x = device(XN)
    to_y = device(YN)

    def rows_of(k, slot, other_core):
        rows = dims[k][0]
        return pl.ds(pl.multiple_of((2 * chip_of(slot) + ((1 - core) if other_core else core)) * rows, rows), rows)

    def load_unit(l, s, k):
        pltpu.make_async_copy(grads[k].at[0, l, rows_of(k, s, True)], stage[k].at[l], ld_unit.at[k, l]).start()
        pltpu.make_async_copy(grads[k].at[0, l, rows_of(k, s, False)], acc[k].at[l, s], ld_unit.at[k, l]).start()

    def remote(src, dst, send, recv, dev):
        return pltpu.make_async_remote_copy(src_ref=src, dst_ref=dst, send_sem=send, recv_sem=recv, device_id=dev, device_id_type=MESH)

    def await_bytes(ref, sem):
        pltpu.make_async_copy(ref, ref, sem).wait()

    first_dev = (to_x, to_y)
    second_dev = (to_y, to_x)
    first_nb = (XN, YN)
    second_nb = (YN, XN)

    def over_rows(k, step, body):
        def run(i, carry):
            body(pl.ds(pl.multiple_of(i * step, step), step))
            return carry

        lax.fori_loop(0, dims[k][0] // step, run, 0)

    def sum_rows(k, body):
        rows, cols = dims[k]
        return lane_fold(lax.fori_loop(
            0, rows // 8, lambda i, c: c + body(pl.ds(pl.multiple_of(i * 8, 8), 8)), jnp.zeros((8, cols), jnp.float32)))

    pairs = [(slots, k) for slots in ((DG, DG), (YN, XN), (XN, YN), (ME, ME)) for k in KIND_ORDER]
    ahead = 3

    def load_pair(slots, k):
        for l in range(LAYERS):
            load_unit(l, slots[l], k)

    for p in pairs[:ahead]:
        load_pair(*p)

    barrier = pltpu.get_barrier_semaphore()
    hops = 3 + jnp.minimum(model, 1) + jnp.minimum(n_model - 1 - model, 1)

    def greet(sem):
        for dev in (partner, to_x, to_y):
            pl.semaphore_signal(sem, inc=1, device_id=dev, device_id_type=MESH)

        @pl.when(model > 0)
        def _():
            pl.semaphore_signal(sem, inc=1, device_id=(model - 1, data), device_id_type=MESH)

        @pl.when(model < n_model - 1)
        def _():
            pl.semaphore_signal(sem, inc=1, device_id=(model + 1, data), device_id_type=MESH)

    greet(barrier)
    pl.semaphore_wait(barrier, hops)
    n_rounds = 2 + n_model - 1
    greet(rounds.at[0])

    def next_round(r):
        pl.semaphore_wait(rounds.at[r], hops)
        if r + 1 < n_rounds:
            greet(rounds.at[r + 1])

    def load_state(k):
        for src, dst in ((weights, wv), (firsts, mv), (seconds, vv)):
            pltpu.make_async_copy(src[k], dst[k], ld_state.at[k]).start()

    def pair_half(g, slots, k):
        for l in range(LAYERS):
            await_bytes(acc[k].at[l, pl.ds(0, 2)], ld_unit.at[k, l])
            s = slots[l]

            def body(r):
                sent[k][l, s, r, :] = stage[k][l, r, :].astype(jnp.bfloat16)

            over_rows(k, 16, body)
            remote(sent[k].at[l, s], got[k].at[l, s], d_send.at[k], d_recv.at[g, k], partner).start()

    def chip_half(g, slots, k):
        await_bytes(got[k].at[pl.ds(0, LAYERS), 0], d_recv.at[g, k])
        for l in range(LAYERS):
            s = slots[l]

            def body(r):
                own = acc[k][l, s, r, :].astype(jnp.bfloat16).astype(jnp.float32)
                acc[k][l, s, r, :] = own + got[k][l, s, r, :].astype(jnp.float32)

            over_rows(k, 16, body)
            if s == DG or s == first_nb[l]:
                t = 0 if s == DG else 1
                remote(acc[k].at[l, s], p1[k].at[l, t], p1_send.at[k], p1_recv.at[t, k], first_dev[l]).start()

    for i in range(len(pairs) + 1):
        if i < len(pairs):
            pair_half(i // KINDS, *pairs[i])
            if i + ahead < len(pairs):
                load_pair(*pairs[i + ahead])
            else:
                for k in (KIND_ORDER[i + ahead - len(pairs)],) + ((KIND_ORDER[ahead],) if i + 1 == len(pairs) else ()):
                    load_state(k)
        if i >= 1:
            chip_half((i - 1) // KINDS, *pairs[i - 1])
        if i >= 4 and i % 2 == 0 and (i - 4) // 2 < n_rounds:
            next_round((i - 4) // 2)

    for k in KIND_ORDER:
        await_bytes(p1[k].at[pl.ds(0, LAYERS), 0], p1_recv.at[0, k])
        for l in range(LAYERS):
            s = second_nb[l]

            def body(r):
                acc[k][l, s, r, :] = acc[k][l, s, r, :] + p1[k][l, 0, r, :]

            over_rows(k, 8, body)
            remote(acc[k].at[l, s], p2[k].at[l], p2_send.at[k], p2_recv.at[k], second_dev[l]).start()

    def share(which, row):
        row_ref[which] = row
        all_ref[which, me] = row
        for dz in sorted(range(n_model), key=lambda z: -min(z, n_model - z)):
            for dd in reversed(range(n_data)):
                if dz or dd:
                    remote(row_ref.at[which], all_ref.at[which, me], ps_send.at[which], ps_recv.at[which],
                           ((model + dz) % n_model, (data + dd) % n_data)).start()

    def shared(which):
        await_bytes(all_ref.at[which, pl.ds(0, n_dev - 1)], ps_recv.at[which])
        return jnp.sum(all_ref[which], axis=0)

    lane = lax.broadcasted_iota(jnp.int32, (1, 128), 1)

    def put(i, part):
        return jnp.where(lane == i, jnp.sum(part, keepdims=True), 0.0)

    def pick(row, i):
        return jnp.sum(jnp.where(lane == i, row, 0.0), axis=1, keepdims=True)

    norms = jnp.zeros((1, 128), jnp.float32)
    for k in KIND_ORDER:
        await_bytes(acc[k].at[pl.ds(0, LAYERS), pl.ds(0, 3)], ld_state.at[k])
        for l in range(LAYERS):
            norms = norms + put(2 * k + l, sum_rows(k, lambda r: wv[k][l, r, :] * wv[k][l, r, :]))
    share(5, norms)

    for k in KIND_ORDER:
        await_bytes(p1[k].at[pl.ds(0, LAYERS), 0], p1_recv.at[1, k])
        for l in range(LAYERS):

            def body(r):
                acc[k][l, ME, r, :] = acc[k][l, ME, r, :] + p1[k][l, 1, r, :]

            over_rows(k, 8, body)
    weight_norms = jnp.sqrt(shared(5))

    grad_sq = jnp.zeros((8, 128), jnp.float32)
    for k in KIND_ORDER:
        await_bytes(p2[k], p2_recv.at[k])
        for l in range(LAYERS):

            def body(r):
                mean = (acc[k][l, ME, r, :] + p2[k][l, r, :]) * (1.0 / n_data)
                acc[k][l, ME, r, :] = mean
                return mean * mean

            grad_sq = grad_sq + sum_rows(k, body)
    share(4, jnp.sum(grad_sq, axis=0, keepdims=True))
    total_sq = jnp.sum(shared(4), axis=1, keepdims=True)
    clip = jnp.minimum(1.0, MAX_NORM / jnp.sqrt(total_sq))
    first_gain = (1.0 - BETA_ONE) * clip
    second_gain = (1.0 - BETA_TWO) * clip * clip
    root_scale = (1.0 - BETA_TWO ** STEP_COUNT) ** 0.5
    hat_scale = root_scale / (1.0 - BETA_ONE ** STEP_COUNT)

    for k in KIND_ORDER:
        squares = jnp.zeros((1, 128), jnp.float32)
        for l in range(LAYERS):

            def body(r):
                mean = acc[k][l, ME, r, :]
                first = BETA_ONE * mv[k][l, r, :] + first_gain * mean
                second = BETA_TWO * vv[k][l, r, :] + second_gain * (mean * mean)
                mv[k][l, r, :] = first
                vv[k][l, r, :] = second
                update = (hat_scale * first) / (jnp.sqrt(second) + ADAM_EPS * root_scale) + DECAY_RATE * wv[k][l, r, :]
                acc[k][l, ME, r, :] = update
                return update * update

            squares = squares + put(2 * k + l, sum_rows(k, body))
        share(k, squares)

    def block(l, s, k):
        return replicas[k].at[l, rows_of(k, s, False)]

    def own_copy(l, second, k):
        return remote(block(l, ME, k), block(l, ME, k), g_send.at[k], g_recv.at[second, k], second_dev[l] if second else first_dev[l])

    def pass_copy(l, k):
        src = block(l, first_nb[l], k)
        return remote(src, src, g_send.at[k], g_recv.at[2, k], second_dev[l])

    def half_copy(l, s, k):
        return remote(block(l, s, k), block(l, s, k), h_send.at[k], h_recv.at[k], partner)

    def await_blocks(i, k):
        await_bytes(got[k].at[pl.ds(0, LAYERS), 0], g_recv.at[i, k])

    for k in KIND_ORDER:
        ratios = weight_norms / jnp.sqrt(shared(k))
        for l in range(LAYERS):
            scale = LEARN_RATE * pick(ratios, 2 * k + l)
            start = pl.multiple_of(data * dims[k][0], dims[k][0])

            def body(r, at):
                fresh = wv[k][l, r, :] - scale * acc[k][l, ME, r, :]
                wv[k][l, r, :] = fresh
                replicas[k][l, pl.ds(pl.multiple_of(start + at, 16), 16), :] = fresh.astype(jnp.bfloat16)

            lax.fori_loop(0, dims[k][0] // 16, lambda i, c: (body(pl.ds(pl.multiple_of(i * 16, 16), 16), i * 16), c)[1], 0)
            own_copy(l, 0, k).start()
    for k in KIND_ORDER:
        for l in range(LAYERS):
            own_copy(l, 1, k).start()
            half_copy(l, ME, k).start()

    last = KIND_ORDER[0]
    for k in KIND_ORDER:
        await_blocks(0, k)
        for l in range(LAYERS):
            if k != last:
                pass_copy(l, k).start()
            half_copy(l, first_nb[l], k).start()
    for l in range(LAYERS):
        pass_copy(l, last).start()
    for k in KIND_ORDER:
        await_blocks(1, k)
        for l in range(LAYERS):
            half_copy(l, second_nb[l], k).start()
    for k in KIND_ORDER[1:] + (last,):
        await_blocks(2, k)
        for l in range(LAYERS):
            half_copy(l, DG, k).start()

    for k in range(KINDS):
        await_bytes(sent[k], d_send.at[k])
        await_bytes(p1[k], p1_send.at[k])
        await_bytes(p2[k], p2_send.at[k])
        await_bytes(got[k].at[pl.ds(0, LAYERS), pl.ds(0, 3)], g_send.at[k])
        await_bytes(got[k], h_send.at[k])
        await_bytes(got[k], h_recv.at[k])
    for which in range(6):
        await_bytes(all_ref.at[which, pl.ds(0, n_dev - 1)], ps_send.at[which])


def write_out(count, *refs):
    srcs, dsts, sems = refs[:count], refs[count:2 * count], refs[2 * count]
    copies = [pltpu.make_async_copy(src, dst, sems.at[i]) for i, (src, dst) in enumerate(zip(srcs, dsts))]
    for c in copies:
        c.start()
    for c in copies:
        c.wait()


def solution(mesh):
    n_model, n_data = mesh.shape["model"], mesh.shape["data"]
    in_specs = []
    for col_split in COLUMN_SPLIT:
        in_specs.extend([grad_spec(col_split), state_spec(col_split), state_spec(col_split), state_spec(col_split)])
    out_specs = tuple([replica_spec(col_split) for col_split in COLUMN_SPLIT] + [state_spec(col_split) for col_split in COLUMN_SPLIT] * 3)

    def device_step(*arrays):
        dims = [arrays[4 * k + 1].shape[1:] for k in range(KINDS)]
        f32, bf16 = jnp.float32, jnp.bfloat16
        out_shape = [jax.ShapeDtypeStruct((LAYERS, n_data * d[0], d[1]), bf16) for d in dims]
        out_shape += [jax.ShapeDtypeStruct((LAYERS,) + tuple(d), f32) for d in dims] * 3

        def each(prefix, dtype):
            return [pltpu.VMEM(prefix + tuple(d), dtype) for d in dims]

        dma = pltpu.SemaphoreType.DMA
        n_dev = n_model * n_data
        scratch = (each((LAYERS, 4), f32) + each((LAYERS,), f32) + each((LAYERS, 4), bf16) + each((LAYERS, 4), bf16)
                   + each((LAYERS, 2), f32) + each((LAYERS,), f32))
        scratch += [pltpu.VMEM((6, 1, 128), f32), pltpu.VMEM((6, n_dev, 1, 128), f32)]
        scratch += [dma((4, 2)), dma((4,)), dma((4,)), dma((4, 4)), dma((4,)), dma((2, 4)), dma((4,)), dma((4,)),
                    dma((4,)), dma((3, 4)), dma((4,)), dma((4,)), dma((6,)), dma((6,)), pltpu.SemaphoreType.REGULAR((n_model + 1,))]
        held = pl.pallas_call(
            functools.partial(kernel, n_model, n_data, dims),
            out_shape=[pltpu.VMEM(o.shape, o.dtype) for o in out_shape],
            in_specs=[pl.BlockSpec(memory_space=pl.ANY)] * 16,
            out_specs=[pl.BlockSpec(memory_space=pltpu.VMEM)] * 16,
            scratch_shapes=scratch,
            compiler_params=pltpu.CompilerParams(collective_id=0, has_side_effects=True, vmem_limit_bytes=COMM_VMEM),
            name="lamb_step",
        )(*arrays)
        held = [pltpu.with_memory_space_constraint(h, pltpu.VMEM) for h in held]
        return tuple(pl.pallas_call(
            functools.partial(write_out, len(out_shape)),
            out_shape=out_shape,
            in_specs=[pl.BlockSpec(memory_space=pltpu.VMEM)] * 16,
            out_specs=[pl.BlockSpec(memory_space=pl.ANY)] * 16,
            scratch_shapes=[dma((16,))],
            compiler_params=pltpu.CompilerParams(vmem_limit_bytes=1 << 20),
            name="write_out",
        )(*held))

    return jax.shard_map(device_step, mesh=mesh, in_specs=tuple(in_specs), out_specs=out_specs, check_vma=False)
```

time: 191 us -> 184 us (0.963)
  Pallas kernels: 190 us -> 183 us
    pallas_call x1, Pallas kernels: 183 us -> 175 us  [device_step(): pl.pallas_call(functools.partial(kernel, n_model, n_data, dims), out_shap...]
where the time goes in v3:
time: 184 us
  Pallas kernels  183 us (99%)
    pallas_call x1, Pallas kernels, device_step(): pl.pallas_call(functools.partial(kernel, n_model, n_data, dims), out_shap...  175 us
    pallas_call x1, Pallas kernels, device_step(): pl.pallas_call(functools.partial(write_out, len(out_shape)), out_shape=ou...  7.56 us

profile of v3, /device:TPU:0, one launch (start us, length us, event | category | flops | bytes accessed | tf_op | source)
XLA Modules:
  0.0 183.7 jit_solution(17681118274499457382)
XLA Ops:
  0.7 175.5 %lamb_step.1 = (bf16[2,1024,768]{2,1,0:T(8,128)(2,1)S(1)}, bf16[2,256,1024]{2,1,0:T(8,128)(2,1)S(1)}, bf16[2,1024,1024]{2,1,0:T(8,128)(2,1)S(1)}, bf16[2,1024,10...) custom-call(f32[1,2,1024,768]{3,2,1,0:T(8,128)} %refs_0_.1, ...), custom_call_target="tpu_custom_call" | custom-call | tf_op jit(solution)/shard_map/lamb_step/pallas_call | solution.py:363
  176.1 7.6 %write_out.1 = (bf16[2,1024,768]{2,1,0:T(8,128)(2,1)}, bf16[2,256,1024]{2,1,0:T(8,128)(2,1)}, bf16[2,1024,1024]{2,1,0:T(8,128)(2,1)}, bf16[2,1024,1024]{2,1,0:T(...) custom-call(bf16[2,1024,768]{2,1,0:T(8,128)(2,1)S(1)} %get-tuple-ele, ...), custom_call_target="tpu_custom_call" | custom-call | tf_op jit(solution)/shard_map/write_out/pallas_call | solution.py:373

commit v4 on v3

--- a/solution.py
+++ b/solution.py
@@ -51,7 +51,7 @@
     scratch = refs[32:]
     acc, stage, sent, got, p1, p2 = (scratch[4 * i:4 * i + 4] for i in range(6))
     (row_ref, all_ref, ld_unit, ld_state, d_send, d_recv, p1_send, p1_recv, p2_send, p2_recv,
-     g_send, g_recv, h_send, h_recv, ps_send, ps_recv, rounds) = scratch[24:]
+     g_send, g_recv, h_send, h_recv, ps_send, ps_recv, raw_sem, rounds, raw_out, raw_in, raw_peer) = scratch[24:]
 
     model = lax.axis_index("model")
     data = lax.axis_index("data")
@@ -110,9 +110,6 @@
         for l in range(LAYERS):
             load_unit(l, slots[l], k)
 
-    for p in pairs[:ahead]:
-        load_pair(*p)
-
     barrier = pltpu.get_barrier_semaphore()
     hops = 3 + jnp.minimum(model, 1) + jnp.minimum(n_model - 1 - model, 1)
 
@@ -129,7 +126,43 @@
             pl.semaphore_signal(sem, inc=1, device_id=(model + 1, data), device_id_type=MESH)
 
     greet(barrier)
+    for p in pairs[:ahead]:
+        load_pair(*p)
+
+    first_kind = KIND_ORDER[0]
+    later_kinds = KIND_ORDER[1:]
+
+    def cast_rows(k, l, s):
+        def body(r):
+            sent[k][l, s, r, :] = stage[k][l, r, :].astype(jnp.bfloat16)
+
+        over_rows(k, 16, body)
+
+    def await_unit(k, l):
+        await_bytes(acc[k].at[l, pl.ds(0, 2)], ld_unit.at[k, l])
+
+    for l in range(LAYERS):
+        await_unit(first_kind, l)
+
+        def body(r):
+            raw_out[l, 0, r, :] = acc[first_kind][l, DG, r, :].astype(jnp.bfloat16)
+            raw_out[l, 1, r, :] = stage[first_kind][l, r, :].astype(jnp.bfloat16)
+
+        over_rows(first_kind, 16, body)
+    load_pair(*pairs[ahead])
+    for l in range(LAYERS):
+        await_unit(pairs[1][1], l)
+        cast_rows(pairs[1][1], l, pairs[1][0][l])
+
     pl.semaphore_wait(barrier, hops)
+    for l in range(LAYERS):
+        remote(raw_out.at[l], raw_in.at[l], raw_sem.at[0], raw_sem.at[1], first_dev[l]).start()
+
+    def pair_send(g, slots, k):
+        for l in range(LAYERS):
+            remote(sent[k].at[l, slots[l]], got[k].at[l, slots[l]], d_send.at[k], d_recv.at[g, k], partner).start()
+
+    pair_send(0, *pairs[1])
     n_rounds = 2 + n_model - 1
     greet(rounds.at[0])
 
@@ -144,14 +177,9 @@
 
     def pair_half(g, slots, k):
         for l in range(LAYERS):
-            await_bytes(acc[k].at[l, pl.ds(0, 2)], ld_unit.at[k, l])
-            s = slots[l]
-
-            def body(r):
-                sent[k][l, s, r, :] = stage[k][l, r, :].astype(jnp.bfloat16)
-
-            over_rows(k, 16, body)
-            remote(sent[k].at[l, s], got[k].at[l, s], d_send.at[k], d_recv.at[g, k], partner).start()
+            await_unit(k, l)
+            cast_rows(k, l, slots[l])
+        pair_send(g, slots, k)
 
     def chip_half(g, slots, k):
         await_bytes(got[k].at[pl.ds(0, LAYERS), 0], d_recv.at[g, k])
@@ -167,28 +195,39 @@
                 t = 0 if s == DG else 1
                 remote(acc[k].at[l, s], p1[k].at[l, t], p1_send.at[k], p1_recv.at[t, k], first_dev[l]).start()
 
-    for i in range(len(pairs) + 1):
+    for i in range(1, len(pairs) + 1):
         if i < len(pairs):
-            pair_half(i // KINDS, *pairs[i])
+            if i >= 2:
+                pair_half(i // KINDS, *pairs[i])
             if i + ahead < len(pairs):
                 load_pair(*pairs[i + ahead])
             else:
                 for k in (KIND_ORDER[i + ahead - len(pairs)],) + ((KIND_ORDER[ahead],) if i + 1 == len(pairs) else ()):
                     load_state(k)
-        if i >= 1:
+        if i >= 2:
             chip_half((i - 1) // KINDS, *pairs[i - 1])
         if i >= 4 and i % 2 == 0 and (i - 4) // 2 < n_rounds:
             next_round((i - 4) // 2)
 
-    for k in KIND_ORDER:
-        await_bytes(p1[k].at[pl.ds(0, LAYERS), 0], p1_recv.at[0, k])
+    await_bytes(raw_in, raw_sem.at[1])
+    for l in range(LAYERS):
+        remote(raw_in.at[l, 1], raw_peer.at[l], raw_sem.at[2], raw_sem.at[3], partner).start()
+    for k in later_kinds + (first_kind,):
+        if k == first_kind:
+            await_bytes(raw_peer, raw_sem.at[3])
+        else:
+            await_bytes(p1[k].at[pl.ds(0, LAYERS), 0], p1_recv.at[0, k])
         for l in range(LAYERS):
             s = second_nb[l]
 
             def body(r):
-                acc[k][l, s, r, :] = acc[k][l, s, r, :] + p1[k][l, 0, r, :]
-
-            over_rows(k, 8, body)
+                if k == first_kind:
+                    come = raw_in[l, 0, r, :].astype(jnp.float32) + raw_peer[l, r, :].astype(jnp.float32)
+                else:
+                    come = p1[k][l, 0, r, :]
+                acc[k][l, s, r, :] = acc[k][l, s, r, :] + come
+
+            over_rows(k, 16, body)
             remote(acc[k].at[l, s], p2[k].at[l], p2_send.at[k], p2_recv.at[k], second_dev[l]).start()
 
     def share(which, row):
@@ -217,7 +256,6 @@
         await_bytes(acc[k].at[pl.ds(0, LAYERS), pl.ds(0, 3)], ld_state.at[k])
         for l in range(LAYERS):
             norms = norms + put(2 * k + l, sum_rows(k, lambda r: wv[k][l, r, :] * wv[k][l, r, :]))
-    share(5, norms)
 
     for k in KIND_ORDER:
         await_bytes(p1[k].at[pl.ds(0, LAYERS), 0], p1_recv.at[1, k])
@@ -227,10 +265,9 @@
                 acc[k][l, ME, r, :] = acc[k][l, ME, r, :] + p1[k][l, 1, r, :]
 
             over_rows(k, 8, body)
-    weight_norms = jnp.sqrt(shared(5))
 
     grad_sq = jnp.zeros((8, 128), jnp.float32)
-    for k in KIND_ORDER:
+    for k in later_kinds + (first_kind,):
         await_bytes(p2[k], p2_recv.at[k])
         for l in range(LAYERS):
 
@@ -249,7 +286,7 @@
     hat_scale = root_scale / (1.0 - BETA_ONE ** STEP_COUNT)
 
     for k in KIND_ORDER:
-        squares = jnp.zeros((1, 128), jnp.float32)
+        squares = norms
         for l in range(LAYERS):
 
             def body(r):
@@ -262,7 +299,7 @@
                 acc[k][l, ME, r, :] = update
                 return update * update
 
-            squares = squares + put(2 * k + l, sum_rows(k, body))
+            squares = squares + put(8 + 2 * k + l, sum_rows(k, body))
         share(k, squares)
 
     def block(l, s, k):
@@ -282,9 +319,9 @@
         await_bytes(got[k].at[pl.ds(0, LAYERS), 0], g_recv.at[i, k])
 
     for k in KIND_ORDER:
-        ratios = weight_norms / jnp.sqrt(shared(k))
-        for l in range(LAYERS):
-            scale = LEARN_RATE * pick(ratios, 2 * k + l)
+        roots = jnp.sqrt(shared(k))
+        for l in range(LAYERS):
+            scale = LEARN_RATE * (pick(roots, 2 * k + l) / pick(roots, 8 + 2 * k + l))
             start = pl.multiple_of(data * dims[k][0], dims[k][0])
 
             def body(r, at):
@@ -318,13 +355,19 @@
             half_copy(l, DG, k).start()
 
     for k in range(KINDS):
-        await_bytes(sent[k], d_send.at[k])
-        await_bytes(p1[k], p1_send.at[k])
+        if k == first_kind:
+            await_bytes(sent[k].at[pl.ds(0, LAYERS), pl.ds(0, 3)], d_send.at[k])
+            await_bytes(p1[k].at[pl.ds(0, LAYERS), 1], p1_send.at[k])
+        else:
+            await_bytes(sent[k], d_send.at[k])
+            await_bytes(p1[k], p1_send.at[k])
         await_bytes(p2[k], p2_send.at[k])
         await_bytes(got[k].at[pl.ds(0, LAYERS), pl.ds(0, 3)], g_send.at[k])
         await_bytes(got[k], h_send.at[k])
         await_bytes(got[k], h_recv.at[k])
-    for which in range(6):
+    await_bytes(raw_in, raw_sem.at[0])
+    await_bytes(raw_peer, raw_sem.at[2])
+    for which in range(5):
         await_bytes(all_ref.at[which, pl.ds(0, n_dev - 1)], ps_send.at[which])
 
 
@@ -357,9 +400,11 @@
         n_dev = n_model * n_data
         scratch = (each((LAYERS, 4), f32) + each((LAYERS,), f32) + each((LAYERS, 4), bf16) + each((LAYERS, 4), bf16)
                    + each((LAYERS, 2), f32) + each((LAYERS,), f32))
-        scratch += [pltpu.VMEM((6, 1, 128), f32), pltpu.VMEM((6, n_dev, 1, 128), f32)]
+        scratch += [pltpu.VMEM((5, 1, 128), f32), pltpu.VMEM((5, n_dev, 1, 128), f32)]
         scratch += [dma((4, 2)), dma((4,)), dma((4,)), dma((4, 4)), dma((4,)), dma((2, 4)), dma((4,)), dma((4,)),
-                    dma((4,)), dma((3, 4)), dma((4,)), dma((4,)), dma((6,)), dma((6,)), pltpu.SemaphoreType.REGULAR((n_model + 1,))]
+                    dma((4,)), dma((3, 4)), dma((4,)), dma((4,)), dma((5,)), dma((5,)), dma((4,)), pltpu.SemaphoreType.REGULAR((n_model + 1,))]
+        first = tuple(dims[KIND_ORDER[0]])
+        scratch += [pltpu.VMEM((LAYERS, 2) + first, bf16), pltpu.VMEM((LAYERS, 2) + first, bf16), pltpu.VMEM((LAYERS,) + first, bf16)]
         held = pl.pallas_call(
             functools.partial(kernel, n_model, n_data, dims),
             out_shape=[pltpu.VMEM(o.shape, o.dtype) for o in out_shape],

time: 184 us -> 181 us (0.984)
  Pallas kernels: 183 us -> 180 us
    pallas_call x1, Pallas kernels: 175 us -> 173 us  [device_step(): pl.pallas_call(functools.partial(kernel, n_model, n_data, dims), out_shap...]
where the time goes in v4:
time: 181 us
  Pallas kernels  180 us (99%)
    pallas_call x1, Pallas kernels, device_step(): pl.pallas_call(functools.partial(kernel, n_model, n_data, dims), out_shap...  173 us
    pallas_call x1, Pallas kernels, device_step(): pl.pallas_call(functools.partial(write_out, len(out_shape)), out_shape=ou...  7.56 us

profile of v4, /device:TPU:0, one launch (start us, length us, event | category | flops | bytes accessed | tf_op | source)
XLA Modules:
  0.0 180.8 jit_solution(17961866466413230024)
XLA Ops:
  0.7 172.5 %lamb_step.1 = (bf16[2,1024,768]{2,1,0:T(8,128)(2,1)S(1)}, bf16[2,256,1024]{2,1,0:T(8,128)(2,1)S(1)}, bf16[2,1024,1024]{2,1,0:T(8,128)(2,1)S(1)}, bf16[2,1024,10...) custom-call(f32[1,2,1024,768]{3,2,1,0:T(8,128)} %refs_0_.1, ...), custom_call_target="tpu_custom_call" | custom-call | tf_op jit(solution)/shard_map/lamb_step/pallas_call | solution.py:408
  173.2 7.6 %write_out.1 = (bf16[2,1024,768]{2,1,0:T(8,128)(2,1)}, bf16[2,256,1024]{2,1,0:T(8,128)(2,1)}, bf16[2,1024,1024]{2,1,0:T(8,128)(2,1)}, bf16[2,1024,1024]{2,1,0:T(...) custom-call(bf16[2,1024,768]{2,1,0:T(8,128)(2,1)S(1)} %get-tuple-ele, ...), custom_call_target="tpu_custom_call" | custom-call | tf_op jit(solution)/shard_map/write_out/pallas_call | solution.py:418

commit v5 on v4

--- a/solution.py
+++ b/solution.py
@@ -14,11 +14,14 @@
 DECAY_RATE = 0.01
 MAX_NORM = 1.0
 STEP_COUNT = 100
+TINY = 1e-36
 COLUMN_SPLIT = (True, False, True, False)
 
 KINDS = 4
 LAYERS = 2
 KIND_ORDER = (1, 0, 2, 3)
+NORM_GROUPS = ((1,), (0,), (2, 3))
+GROUPS = len(NORM_GROUPS)
 ME, XN, YN, DG = 0, 1, 2, 3
 MESH = pl.DeviceIdType.MESH
 COMM_VMEM = 42 << 20
@@ -51,7 +54,8 @@
     scratch = refs[32:]
     acc, stage, sent, got, p1, p2 = (scratch[4 * i:4 * i + 4] for i in range(6))
     (row_ref, all_ref, ld_unit, ld_state, d_send, d_recv, p1_send, p1_recv, p2_send, p2_recv,
-     g_send, g_recv, h_send, h_recv, ps_send, ps_recv, raw_sem, rounds, raw_out, raw_in, raw_peer) = scratch[24:]
+     g_send, g_recv, h_send, h_recv, ps_send, ps_recv, raw_sem, early_sem, rounds,
+     raw_out, raw_in, raw_peer, early_w, early_u) = scratch[24:]
 
     model = lax.axis_index("model")
     data = lax.axis_index("data")
@@ -100,8 +104,13 @@
 
     def sum_rows(k, body):
         rows, cols = dims[k]
-        return lane_fold(lax.fori_loop(
-            0, rows // 8, lambda i, c: c + body(pl.ds(pl.multiple_of(i * 8, 8), 8)), jnp.zeros((8, cols), jnp.float32)))
+
+        def run(i, carry):
+            r = pl.ds(pl.multiple_of(i * 8, 8), 8)
+            return tuple(carry[l] + body(l, r) for l in range(LAYERS))
+
+        sums = lax.fori_loop(0, rows // 8, run, (jnp.zeros((8, cols), jnp.float32),) * LAYERS)
+        return [lane_fold(x) for x in sums]
 
     pairs = [(slots, k) for slots in ((DG, DG), (YN, XN), (XN, YN), (ME, ME)) for k in KIND_ORDER]
     ahead = 3
@@ -111,12 +120,9 @@
             load_unit(l, slots[l], k)
 
     barrier = pltpu.get_barrier_semaphore()
-    hops = 3 + jnp.minimum(model, 1) + jnp.minimum(n_model - 1 - model, 1)
-
-    def greet(sem):
-        for dev in (partner, to_x, to_y):
-            pl.semaphore_signal(sem, inc=1, device_id=dev, device_id_type=MESH)
-
+    z_hops = jnp.minimum(model, 1) + jnp.minimum(n_model - 1 - model, 1)
+
+    def greet_z(sem):
         @pl.when(model > 0)
         def _():
             pl.semaphore_signal(sem, inc=1, device_id=(model - 1, data), device_id_type=MESH)
@@ -125,7 +131,9 @@
         def _():
             pl.semaphore_signal(sem, inc=1, device_id=(model + 1, data), device_id_type=MESH)
 
-    greet(barrier)
+    for dev in (partner, to_x, to_y):
+        pl.semaphore_signal(barrier, inc=1, device_id=dev, device_id_type=MESH)
+    greet_z(barrier)
     for p in pairs[:ahead]:
         load_pair(*p)
 
@@ -154,7 +162,7 @@
         await_unit(pairs[1][1], l)
         cast_rows(pairs[1][1], l, pairs[1][0][l])
 
-    pl.semaphore_wait(barrier, hops)
+    pl.semaphore_wait(barrier, 3 + z_hops)
     for l in range(LAYERS):
         remote(raw_out.at[l], raw_in.at[l], raw_sem.at[0], raw_sem.at[1], first_dev[l]).start()
 
@@ -163,13 +171,21 @@
             remote(sent[k].at[l, slots[l]], got[k].at[l, slots[l]], d_send.at[k], d_recv.at[g, k], partner).start()
 
     pair_send(0, *pairs[1])
-    n_rounds = 2 + n_model - 1
-    greet(rounds.at[0])
+    axes = ("z",) * (n_model - 2) + ("core", "x", "y")
+    n_rounds = len(axes)
+
+    def greet_round(r):
+        if axes[r] == "z":
+            greet_z(rounds.at[r])
+        else:
+            pl.semaphore_signal(rounds.at[r], inc=1, device_id={"core": partner, "x": to_x, "y": to_y}[axes[r]], device_id_type=MESH)
+
+    greet_round(0)
 
     def next_round(r):
-        pl.semaphore_wait(rounds.at[r], hops)
+        pl.semaphore_wait(rounds.at[r], z_hops if axes[r] == "z" else 1)
         if r + 1 < n_rounds:
-            greet(rounds.at[r + 1])
+            greet_round(r + 1)
 
     def load_state(k):
         for src, dst in ((weights, wv), (firsts, mv), (seconds, vv)):
@@ -254,8 +270,8 @@
     norms = jnp.zeros((1, 128), jnp.float32)
     for k in KIND_ORDER:
         await_bytes(acc[k].at[pl.ds(0, LAYERS), pl.ds(0, 3)], ld_state.at[k])
-        for l in range(LAYERS):
-            norms = norms + put(2 * k + l, sum_rows(k, lambda r: wv[k][l, r, :] * wv[k][l, r, :]))
+        for l, part in enumerate(sum_rows(k, lambda l, r: wv[k][l, r, :] * wv[k][l, r, :])):
+            norms = norms + put(2 * k + l, part)
 
     for k in KIND_ORDER:
         await_bytes(p1[k].at[pl.ds(0, LAYERS), 0], p1_recv.at[1, k])
@@ -269,38 +285,51 @@
     grad_sq = jnp.zeros((8, 128), jnp.float32)
     for k in later_kinds + (first_kind,):
         await_bytes(p2[k], p2_recv.at[k])
-        for l in range(LAYERS):
-
-            def body(r):
-                mean = (acc[k][l, ME, r, :] + p2[k][l, r, :]) * (1.0 / n_data)
-                acc[k][l, ME, r, :] = mean
-                return mean * mean
-
-            grad_sq = grad_sq + sum_rows(k, body)
-    share(4, jnp.sum(grad_sq, axis=0, keepdims=True))
-    total_sq = jnp.sum(shared(4), axis=1, keepdims=True)
+
+        def body(l, r):
+            mean = (acc[k][l, ME, r, :] + p2[k][l, r, :]) * (1.0 / n_data)
+            acc[k][l, ME, r, :] = mean
+            return mean * mean
+
+        for part in sum_rows(k, body):
+            grad_sq = grad_sq + part
+    share(GROUPS, jnp.sum(grad_sq, axis=0, keepdims=True))
+
+    for l in range(LAYERS):
+        remote(wv[first_kind].at[l], early_w.at[l], early_sem.at[0], early_sem.at[1], first_dev[l]).start()
+    total_sq = jnp.sum(shared(GROUPS), axis=1, keepdims=True)
     clip = jnp.minimum(1.0, MAX_NORM / jnp.sqrt(total_sq))
     first_gain = (1.0 - BETA_ONE) * clip
     second_gain = (1.0 - BETA_TWO) * clip * clip
     root_scale = (1.0 - BETA_TWO ** STEP_COUNT) ** 0.5
     hat_scale = root_scale / (1.0 - BETA_ONE ** STEP_COUNT)
 
-    for k in KIND_ORDER:
+    def updates(k):
+        def body(l, r):
+            mean = acc[k][l, ME, r, :]
+            first = BETA_ONE * mv[k][l, r, :] + first_gain * mean
+            second = BETA_TWO * vv[k][l, r, :] + second_gain * (mean * mean)
+            mv[k][l, r, :] = first
+            vv[k][l, r, :] = second
+            root = jnp.maximum(second, TINY)
+            root = root * lax.rsqrt(root)
+            update = (hat_scale * first) / (root + ADAM_EPS * root_scale) + DECAY_RATE * wv[k][l, r, :]
+            acc[k][l, ME, r, :] = update
+            return update * update
+
+        return sum_rows(k, body)
+
+    for g, kinds in enumerate(NORM_GROUPS):
         squares = norms
-        for l in range(LAYERS):
-
-            def body(r):
-                mean = acc[k][l, ME, r, :]
-                first = BETA_ONE * mv[k][l, r, :] + first_gain * mean
-                second = BETA_TWO * vv[k][l, r, :] + second_gain * (mean * mean)
-                mv[k][l, r, :] = first
-                vv[k][l, r, :] = second
-                update = (hat_scale * first) / (jnp.sqrt(second) + ADAM_EPS * root_scale) + DECAY_RATE * wv[k][l, r, :]
-                acc[k][l, ME, r, :] = update
-                return update * update
-
-            squares = squares + put(8 + 2 * k + l, sum_rows(k, body))
-        share(k, squares)
+        for k in kinds:
+            for l, part in enumerate(updates(k)):
+                squares = squares + put(8 + 2 * k + l, part)
+        share(g, squares)
+        if g < 2:
+            half = dims[first_kind][0] // 2
+            piece = pl.ds(g * half, half)
+            for l in range(LAYERS):
+                remote(acc[first_kind].at[l, ME, piece], early_u.at[l, piece], early_sem.at[2], early_sem.at[3], first_dev[l]).start()
 
     def block(l, s, k):
         return replicas[k].at[l, rows_of(k, s, False)]
@@ -318,38 +347,58 @@
     def await_blocks(i, k):
         await_bytes(got[k].at[pl.ds(0, LAYERS), 0], g_recv.at[i, k])
 
-    for k in KIND_ORDER:
-        roots = jnp.sqrt(shared(k))
-        for l in range(LAYERS):
-            scale = LEARN_RATE * (pick(roots, 2 * k + l) / pick(roots, 8 + 2 * k + l))
-            start = pl.multiple_of(data * dims[k][0], dims[k][0])
-
-            def body(r, at):
-                fresh = wv[k][l, r, :] - scale * acc[k][l, ME, r, :]
-                wv[k][l, r, :] = fresh
-                replicas[k][l, pl.ds(pl.multiple_of(start + at, 16), 16), :] = fresh.astype(jnp.bfloat16)
-
-            lax.fori_loop(0, dims[k][0] // 16, lambda i, c: (body(pl.ds(pl.multiple_of(i * 16, 16), 16), i * 16), c)[1], 0)
-            own_copy(l, 0, k).start()
-    for k in KIND_ORDER:
+    def new_rows(k, l, s, scale, take):
+        start = pl.multiple_of((2 * chip_of(s) + core) * dims[k][0], dims[k][0])
+
+        def run(i, carry):
+            at = i * 16
+            replicas[k][l, pl.ds(pl.multiple_of(start + at, 16), 16), :] = take(pl.ds(pl.multiple_of(at, 16), 16), scale).astype(jnp.bfloat16)
+            return carry
+
+        lax.fori_loop(0, dims[k][0] // 16, run, 0)
+
+    for g, kinds in enumerate(NORM_GROUPS):
+        roots = jnp.sqrt(shared(g))
+        scales = {(k, l): LEARN_RATE * (pick(roots, 2 * k + l) / pick(roots, 8 + 2 * k + l)) for k in kinds for l in range(LAYERS)}
+        if g == 0:
+            await_bytes(early_w, early_sem.at[0])
+        for k in kinds:
+            for l in range(LAYERS):
+
+                def fresh_rows(r, scale):
+                    fresh = wv[k][l, r, :] - scale * acc[k][l, ME, r, :]
+                    wv[k][l, r, :] = fresh
+                    return fresh
+
+                new_rows(k, l, ME, scales[k, l], fresh_rows)
+                own_copy(l, 1 if g == 0 else 0, k).start()
+        if g == 0:
+            first_scales = scales
+            for l in range(LAYERS):
+                half_copy(l, ME, first_kind).start()
+
+    for k in later_kinds:
         for l in range(LAYERS):
             own_copy(l, 1, k).start()
             half_copy(l, ME, k).start()
 
-    last = KIND_ORDER[0]
-    for k in KIND_ORDER:
+    await_bytes(early_w, early_sem.at[1])
+    await_bytes(early_u, early_sem.at[3])
+    for l in range(LAYERS):
+        new_rows(first_kind, l, first_nb[l], first_scales[first_kind, l], lambda r, scale: early_w[l, r, :] - scale * early_u[l, r, :])
+        half_copy(l, first_nb[l], first_kind).start()
+    for k in later_kinds:
         await_blocks(0, k)
         for l in range(LAYERS):
-            if k != last:
-                pass_copy(l, k).start()
+            pass_copy(l, k).start()
             half_copy(l, first_nb[l], k).start()
     for l in range(LAYERS):
-        pass_copy(l, last).start()
+        pass_copy(l, first_kind).start()
     for k in KIND_ORDER:
         await_blocks(1, k)
         for l in range(LAYERS):
             half_copy(l, second_nb[l], k).start()
-    for k in KIND_ORDER[1:] + (last,):
+    for k in later_kinds + (first_kind,):
         await_blocks(2, k)
         for l in range(LAYERS):
             half_copy(l, DG, k).start()
@@ -362,12 +411,13 @@
             await_bytes(sent[k], d_send.at[k])
             await_bytes(p1[k], p1_send.at[k])
         await_bytes(p2[k], p2_send.at[k])
-        await_bytes(got[k].at[pl.ds(0, LAYERS), pl.ds(0, 3)], g_send.at[k])
+        await_bytes(got[k].at[pl.ds(0, LAYERS), pl.ds(0, 2 if k == first_kind else 3)], g_send.at[k])
         await_bytes(got[k], h_send.at[k])
         await_bytes(got[k], h_recv.at[k])
     await_bytes(raw_in, raw_sem.at[0])
     await_bytes(raw_peer, raw_sem.at[2])
-    for which in range(5):
+    await_bytes(early_u, early_sem.at[2])
+    for which in range(GROUPS + 1):
         await_bytes(all_ref.at[which, pl.ds(0, n_dev - 1)], ps_send.at[which])
 
 
@@ -400,11 +450,12 @@
         n_dev = n_model * n_data
         scratch = (each((LAYERS, 4), f32) + each((LAYERS,), f32) + each((LAYERS, 4), bf16) + each((LAYERS, 4), bf16)
                    + each((LAYERS, 2), f32) + each((LAYERS,), f32))
-        scratch += [pltpu.VMEM((5, 1, 128), f32), pltpu.VMEM((5, n_dev, 1, 128), f32)]
+        scratch += [pltpu.VMEM((GROUPS + 1, 1, 128), f32), pltpu.VMEM((GROUPS + 1, n_dev, 1, 128), f32)]
         scratch += [dma((4, 2)), dma((4,)), dma((4,)), dma((4, 4)), dma((4,)), dma((2, 4)), dma((4,)), dma((4,)),
-                    dma((4,)), dma((3, 4)), dma((4,)), dma((4,)), dma((5,)), dma((5,)), dma((4,)), pltpu.SemaphoreType.REGULAR((n_model + 1,))]
+                    dma((4,)), dma((3, 4)), dma((4,)), dma((4,)), dma((GROUPS + 1,)), dma((GROUPS + 1,)), dma((4,)), dma((4,)), pltpu.SemaphoreType.REGULAR((n_model + 1,))]
         first = tuple(dims[KIND_ORDER[0]])
         scratch += [pltpu.VMEM((LAYERS, 2) + first, bf16), pltpu.VMEM((LAYERS, 2) + first, bf16), pltpu.VMEM((LAYERS,) + first, bf16)]
+        scratch += [pltpu.VMEM((LAYERS,) + first, f32)] * 2
         held = pl.pallas_call(
             functools.partial(kernel, n_model, n_data, dims),
             out_shape=[pltpu.VMEM(o.shape, o.dtype) for o in out_shape],

time: 181 us -> 179 us (0.989)
  Pallas kernels: 180 us -> 178 us
where the time goes in v5:
time: 179 us
  Pallas kernels  178 us (99%)
    pallas_call x1, Pallas kernels, device_step(): pl.pallas_call(functools.partial(kernel, n_model, n_data, dims), out_shap...  171 us
    pallas_call x1, Pallas kernels, device_step(): pl.pallas_call(functools.partial(write_out, len(out_shape)), out_shape=ou...  7.56 us

profile of v5, /device:TPU:0, one launch (start us, length us, event | category | flops | bytes accessed | tf_op | source)
XLA Modules:
  0.0 179.0 jit_solution(5243743381383139077)
XLA Ops:
  0.7 170.8 %lamb_step.1 = (bf16[2,1024,768]{2,1,0:T(8,128)(2,1)S(1)}, bf16[2,256,1024]{2,1,0:T(8,128)(2,1)S(1)}, bf16[2,1024,1024]{2,1,0:T(8,128)(2,1)S(1)}, bf16[2,1024,10...) custom-call(f32[1,2,1024,768]{3,2,1,0:T(8,128)} %refs_0_.1, ...), custom_call_target="tpu_custom_call" | custom-call | tf_op jit(solution)/shard_map/lamb_step/pallas_call | solution.py:459
  171.5 7.6 %write_out.1 = (bf16[2,1024,768]{2,1,0:T(8,128)(2,1)}, bf16[2,256,1024]{2,1,0:T(8,128)(2,1)}, bf16[2,1024,1024]{2,1,0:T(8,128)(2,1)}, bf16[2,1024,1024]{2,1,0:T(...) custom-call(bf16[2,1024,768]{2,1,0:T(8,128)(2,1)S(1)} %get-tuple-ele, ...), custom_call_target="tpu_custom_call" | custom-call | tf_op jit(solution)/shard_map/write_out/pallas_call | solution.py:469

commit v6 on v5

--- a/solution.py
+++ b/solution.py
@@ -54,7 +54,7 @@
     scratch = refs[32:]
     acc, stage, sent, got, p1, p2 = (scratch[4 * i:4 * i + 4] for i in range(6))
     (row_ref, all_ref, ld_unit, ld_state, d_send, d_recv, p1_send, p1_recv, p2_send, p2_recv,
-     g_send, g_recv, h_send, h_recv, ps_send, ps_recv, raw_sem, early_sem, rounds,
+     g_send, g_recv, h_send, h_recv, ps_send, ps_recv, raw_sem, early_sem, tail_sem, rounds,
      raw_out, raw_in, raw_peer, early_w, early_u) = scratch[24:]
 
     model = lax.axis_index("model")
@@ -252,7 +252,7 @@
         for dz in sorted(range(n_model), key=lambda z: -min(z, n_model - z)):
             for dd in reversed(range(n_data)):
                 if dz or dd:
-                    remote(row_ref.at[which], all_ref.at[which, me], ps_send.at[which], ps_recv.at[which],
+                    remote(row_ref.at[which], all_ref.at[which, me], ps_send.at[0], ps_recv.at[which],
                            ((model + dz) % n_model, (data + dd) % n_data)).start()
 
     def shared(which):
@@ -390,18 +390,43 @@
     for k in later_kinds:
         await_blocks(0, k)
         for l in range(LAYERS):
-            pass_copy(l, k).start()
+            if k != later_kinds[0]:
+                pass_copy(l, k).start()
             half_copy(l, first_nb[l], k).start()
     for l in range(LAYERS):
-        pass_copy(l, first_kind).start()
+        pass_copy(l, later_kinds[0]).start()
+    half = dims[first_kind][0] // 2
+
+    def part_block(l, s, upper):
+        start = pl.multiple_of((2 * chip_of(s) + core) * dims[first_kind][0] + upper * half, half)
+        return replicas[first_kind].at[l, pl.ds(start, half)]
+
+    def last_copy(l, other_core):
+        src = part_block(l, first_nb[l], 1)
+        send = h_send if other_core else g_send
+        return remote(src, src, send.at[first_kind], tail_sem.at[other_core], device(second_nb[l], bool(other_core)))
+
+    for l in range(LAYERS):
+        src = part_block(l, first_nb[l], 0)
+        remote(src, src, g_send.at[first_kind], g_recv.at[2, first_kind], second_dev[l]).start()
+    for l in range(LAYERS):
+        for other_core in range(2):
+            last_copy(l, other_core).start()
     for k in KIND_ORDER:
         await_blocks(1, k)
         for l in range(LAYERS):
             half_copy(l, second_nb[l], k).start()
-    for k in later_kinds + (first_kind,):
+    for k in later_kinds[1:] + later_kinds[:1]:
         await_blocks(2, k)
         for l in range(LAYERS):
             half_copy(l, DG, k).start()
+    half_bytes = got[first_kind].at[pl.ds(0, LAYERS), 0, pl.ds(0, half)]
+    await_bytes(half_bytes, g_recv.at[2, first_kind])
+    for l in range(LAYERS):
+        src = part_block(l, DG, 0)
+        remote(src, src, h_send.at[first_kind], h_recv.at[first_kind], partner).start()
+    for other_core in range(2):
+        await_bytes(half_bytes, tail_sem.at[other_core])
 
     for k in range(KINDS):
         if k == first_kind:
@@ -413,21 +438,27 @@
         await_bytes(p2[k], p2_send.at[k])
         await_bytes(got[k].at[pl.ds(0, LAYERS), pl.ds(0, 2 if k == first_kind else 3)], g_send.at[k])
         await_bytes(got[k], h_send.at[k])
-        await_bytes(got[k], h_recv.at[k])
+        if k == first_kind:
+            await_bytes(replicas[2].at[0, pl.ds(0, LAYERS * 7 * half)], h_recv.at[k])
+        else:
+            await_bytes(got[k], h_recv.at[k])
     await_bytes(raw_in, raw_sem.at[0])
     await_bytes(raw_peer, raw_sem.at[2])
     await_bytes(early_u, early_sem.at[2])
-    for which in range(GROUPS + 1):
-        await_bytes(all_ref.at[which, pl.ds(0, n_dev - 1)], ps_send.at[which])
+    await_bytes(all_ref.at[pl.ds(0, GROUPS + 1), pl.ds(0, n_dev - 1)], ps_send.at[0])
 
 
 def write_out(count, *refs):
     srcs, dsts, sems = refs[:count], refs[count:2 * count], refs[2 * count]
-    copies = [pltpu.make_async_copy(src, dst, sems.at[i]) for i, (src, dst) in enumerate(zip(srcs, dsts))]
-    for c in copies:
-        c.start()
-    for c in copies:
-        c.wait()
+    pieces = 4
+    for i, (src, dst) in enumerate(zip(srcs, dsts)):
+        rows = src.shape[1] // pieces
+        for l in range(LAYERS):
+            for h in range(pieces):
+                part = (l, pl.ds(h * rows, rows))
+                pltpu.make_async_copy(src.at[part], dst.at[part], sems.at[i]).start()
+    for i, (src, dst) in enumerate(zip(srcs, dsts)):
+        pltpu.make_async_copy(src, dst, sems.at[i]).wait()
 
 
 def solution(mesh):
@@ -452,7 +483,7 @@
                    + each((LAYERS, 2), f32) + each((LAYERS,), f32))
         scratch += [pltpu.VMEM((GROUPS + 1, 1, 128), f32), pltpu.VMEM((GROUPS + 1, n_dev, 1, 128), f32)]
         scratch += [dma((4, 2)), dma((4,)), dma((4,)), dma((4, 4)), dma((4,)), dma((2, 4)), dma((4,)), dma((4,)),
-                    dma((4,)), dma((3, 4)), dma((4,)), dma((4,)), dma((GROUPS + 1,)), dma((GROUPS + 1,)), dma((4,)), dma((4,)), pltpu.SemaphoreType.REGULAR((n_model + 1,))]
+                    dma((4,)), dma((3, 4)), dma((4,)), dma((4,)), dma((1,)), dma((GROUPS + 1,)), dma((4,)), dma((4,)), dma((2,)), pltpu.SemaphoreType.REGULAR((n_model + 1,))]
         first = tuple(dims[KIND_ORDER[0]])
         scratch += [pltpu.VMEM((LAYERS, 2) + first, bf16), pltpu.VMEM((LAYERS, 2) + first, bf16), pltpu.VMEM((LAYERS,) + first, bf16)]
         scratch += [pltpu.VMEM((LAYERS,) + first, f32)] * 2

time: 179 us -> 179 us (level)
  no operation moved by 1% of the time
where the time goes in v6:
time: 179 us
  Pallas kernels  178 us (99%)
    pallas_call x1, Pallas kernels, device_step(): pl.pallas_call(functools.partial(kernel, n_model, n_data, dims), out_shap...  171 us
    pallas_call x1, Pallas kernels, device_step(): pl.pallas_call(functools.partial(write_out, len(out_shape)), out_shape=ou...  7.48 us

profile of v6, /device:TPU:0, one launch (start us, length us, event | category | flops | bytes accessed | tf_op | source)
XLA Modules:
  0.0 178.8 jit_solution(5233494470500258209)
XLA Ops:
  0.7 170.6 %lamb_step.1 = (bf16[2,1024,768]{2,1,0:T(8,128)(2,1)S(1)}, bf16[2,256,1024]{2,1,0:T(8,128)(2,1)S(1)}, bf16[2,1024,1024]{2,1,0:T(8,128)(2,1)S(1)}, bf16[2,1024,10...) custom-call(f32[1,2,1024,768]{3,2,1,0:T(8,128)} %refs_0_.1, ...), custom_call_target="tpu_custom_call" | custom-call | tf_op jit(solution)/shard_map/lamb_step/pallas_call | solution.py:490
  171.3 7.5 %write_out.1 = (bf16[2,1024,768]{2,1,0:T(8,128)(2,1)}, bf16[2,256,1024]{2,1,0:T(8,128)(2,1)}, bf16[2,1024,1024]{2,1,0:T(8,128)(2,1)}, bf16[2,1024,1024]{2,1,0:T(...) custom-call(bf16[2,1024,768]{2,1,0:T(8,128)(2,1)S(1)} %get-tuple-ele, ...), custom_call_target="tpu_custom_call" | custom-call | tf_op jit(solution)/shard_map/write_out/pallas_call | solution.py:500

commit v7 on v6

--- a/solution.py
+++ b/solution.py
@@ -257,7 +257,8 @@
 
     def shared(which):
         await_bytes(all_ref.at[which, pl.ds(0, n_dev - 1)], ps_recv.at[which])
-        return jnp.sum(all_ref[which], axis=0)
+        parts = [jnp.sum(all_ref[which, pl.ds(i, n_dev // 4)], axis=0) for i in range(0, n_dev, n_dev // 4)]
+        return (parts[0] + parts[1]) + (parts[2] + parts[3])
 
     lane = lax.broadcasted_iota(jnp.int32, (1, 128), 1)
 
@@ -311,8 +312,8 @@
             second = BETA_TWO * vv[k][l, r, :] + second_gain * (mean * mean)
             mv[k][l, r, :] = first
             vv[k][l, r, :] = second
-            root = jnp.maximum(second, TINY)
-            root = root * lax.rsqrt(root)
+            shifted = second + TINY
+            root = shifted * lax.rsqrt(shifted)
             update = (hat_scale * first) / (root + ADAM_EPS * root_scale) + DECAY_RATE * wv[k][l, r, :]
             acc[k][l, ME, r, :] = update
             return update * update

time: 179 us -> 179 us (level)
  no operation moved by 1% of the time
where the time goes in v7:
time: 179 us
  Pallas kernels  178 us (99%)
    pallas_call x1, Pallas kernels, device_step(): pl.pallas_call(functools.partial(kernel, n_model, n_data, dims), out_shap...  171 us
    pallas_call x1, Pallas kernels, device_step(): pl.pallas_call(functools.partial(write_out, len(out_shape)), out_shape=ou...  7.48 us

profile of v7, /device:TPU:0, one launch (start us, length us, event | category | flops | bytes accessed | tf_op | source)
XLA Modules:
  0.0 178.7 jit_solution(670978323240576907)
XLA Ops:
  0.7 170.6 %lamb_step.1 = (bf16[2,1024,768]{2,1,0:T(8,128)(2,1)S(1)}, bf16[2,256,1024]{2,1,0:T(8,128)(2,1)S(1)}, bf16[2,1024,1024]{2,1,0:T(8,128)(2,1)S(1)}, bf16[2,1024,10...) custom-call(f32[1,2,1024,768]{3,2,1,0:T(8,128)} %refs_0_.1, ...), custom_call_target="tpu_custom_call" | custom-call | tf_op jit(solution)/shard_map/lamb_step/pallas_call | solution.py:491
  171.2 7.5 %write_out.1 = (bf16[2,1024,768]{2,1,0:T(8,128)(2,1)}, bf16[2,256,1024]{2,1,0:T(8,128)(2,1)}, bf16[2,1024,1024]{2,1,0:T(8,128)(2,1)}, bf16[2,1024,1024]{2,1,0:T(...) custom-call(bf16[2,1024,768]{2,1,0:T(8,128)(2,1)S(1)} %get-tuple-ele, ...), custom_call_target="tpu_custom_call" | custom-call | tf_op jit(solution)/shard_map/write_out/pallas_call | solution.py:501

commit v8 on v7

--- a/solution.py
+++ b/solution.py
@@ -250,7 +250,7 @@
         row_ref[which] = row
         all_ref[which, me] = row
         for dz in sorted(range(n_model), key=lambda z: -min(z, n_model - z)):
-            for dd in reversed(range(n_data)):
+            for dd in (3, 0, 2, 7, 4, 1, 5, 6):
                 if dz or dd:
                     remote(row_ref.at[which], all_ref.at[which, me], ps_send.at[0], ps_recv.at[which],
                            ((model + dz) % n_model, (data + dd) % n_data)).start()

time: 179 us -> 179 us (level)
  no operation moved by 1% of the time
where the time goes in v8:
time: 179 us
  Pallas kernels  178 us (99%)
    pallas_call x1, Pallas kernels, device_step(): pl.pallas_call(functools.partial(kernel, n_model, n_data, dims), out_shap...  171 us
    pallas_call x1, Pallas kernels, device_step(): pl.pallas_call(functools.partial(write_out, len(out_shape)), out_shape=ou...  7.48 us

profile of v8, /device:TPU:0, one launch (start us, length us, event | category | flops | bytes accessed | tf_op | source)
XLA Modules:
  0.0 178.6 jit_solution(14844433175092827539)
XLA Ops:
  0.7 170.5 %lamb_step.1 = (bf16[2,1024,768]{2,1,0:T(8,128)(2,1)S(1)}, bf16[2,256,1024]{2,1,0:T(8,128)(2,1)S(1)}, bf16[2,1024,1024]{2,1,0:T(8,128)(2,1)S(1)}, bf16[2,1024,10...) custom-call(f32[1,2,1024,768]{3,2,1,0:T(8,128)} %refs_0_.1, ...), custom_call_target="tpu_custom_call" | custom-call | tf_op jit(solution)/shard_map/lamb_step/pallas_call | solution.py:491
  171.2 7.5 %write_out.1 = (bf16[2,1024,768]{2,1,0:T(8,128)(2,1)}, bf16[2,256,1024]{2,1,0:T(8,128)(2,1)}, bf16[2,1024,1024]{2,1,0:T(8,128)(2,1)}, bf16[2,1024,1024]{2,1,0:T(...) custom-call(bf16[2,1024,768]{2,1,0:T(8,128)(2,1)S(1)} %get-tuple-ele, ...), custom_call_target="tpu_custom_call" | custom-call | tf_op jit(solution)/shard_map/write_out/pallas_call | solution.py:501
